TPU v7x, 512 devices: a whole 4x8x8 slice. The times are simulated.
512 devices in a mesh: fsdp: 64 (over z, y_hi, core), tensor: 8 (over y_lo, x).
Axes of the slice: x: 4, y: 8 (y_hi: 4, y_lo: 2; y = y_hi * 2 + y_lo), z: 8, core: 2. Of those that a mesh axis runs over, the one named last changes fastest.
Arguments:
- hidden: bfloat16 [256, 8192], P(None, 'fsdp'), may hold values from -128 to 128
- head_weight: bfloat16 [65536, 8192], P('tensor', 'fsdp'), may hold values from -1 to 1
- targets: int32 [256], replicated, may hold values from 0 to 65535
Outputs:
- logprob: float32 [256], replicated
- greedy_gap: float32 [256], replicated
All inputs are finite; a program needn't handle non-finite values.
Results may differ from a plain program's by a relative error of at most 0.0003.
Values may be sent and summed in bfloat16 or wider, within the bound.
No kernel may reach another device: no remote copies, remote signals or barrier semaphores. Data moves between devices by JAX's collectives and lax.ppermute only.
A program may use at most 64 MiB of HBM per device.

v0:
```python
import jax
import jax.numpy as jnp
from jax import lax
from jax.sharding import Mesh
from jax.sharding import PartitionSpec as P

FSDP = ("fsdp_0", "fsdp_1", "fsdp_2")
TENSOR = ("tensor_0", "tensor_1")
FSDP_TENSOR = ("fsdp_0", "fsdp_1", "fsdp_2", "tensor_0", "tensor_1")


def all_in_one(array, axis):
    leaves = jax.tree.leaves(array)
    sequence = sorted(range(len(leaves)), key=lambda k: -leaves[k].size)
    width = (1, *leaves[sequence[0]].shape)[-1]
    lines = [
        jnp.pad(leaves[k].reshape(-1), (0, -leaves[k].size % width)).reshape(-1, width)
        for k in sequence
    ]
    both, at, found = (lax.all_gather(jnp.concatenate(lines), axis), 0, {})
    for k, line in zip(sequence, lines):
        piece = both[:, at : at + len(line)].reshape(len(both), -1)
        found[k] = piece[:, : leaves[k].size].reshape(-1, *leaves[k].shape)
        at += len(line)
    numbers = iter(range(len(leaves)))
    return jax.tree.map(lambda _: found[next(numbers)], array)


def joined_all(array, axes, combine):
    for axis in axes:
        pieces = all_in_one(array, axis)
        array = jax.tree.map(lambda part: part[0], pieces)
        for k in range(1, lax.axis_size(axis)):
            array = combine(array, jax.tree.map(lambda part: part[k], pieces))
    return array


def contract_rows(left, right):
    return lax.dot_general(
        left, right, (((1,), (1,)), ((), ())), preferred_element_type=jnp.float32
    )


def combine_stats(earlier, later):
    peak_one, expsum_one, target_one = earlier
    peak_two, expsum_two, target_two = later
    new_peak = jnp.maximum(peak_one, peak_two)
    expsum = expsum_one * jnp.exp(peak_one - new_peak) + expsum_two * jnp.exp(peak_two - new_peak)
    return (new_peak, expsum, target_one + target_two)


def per_device(hidden, head_weight, targets):
    fsdp_index = lax.axis_index(FSDP)
    regrouped = lax.all_to_all(head_weight, FSDP, split_axis=0, concat_axis=1, tiled=True)
    vocab_rows = regrouped.shape[0]
    offset = lax.axis_index(TENSOR) * (vocab_rows * lax.axis_size(FSDP)) + fsdp_index * vocab_rows
    gathered = lax.all_gather(hidden, FSDP, axis=1, tiled=True)
    logits = contract_rows(gathered, regrouped)
    vocab_ids = offset + jnp.arange(vocab_rows, dtype=jnp.int32)
    matches = vocab_ids[None, :] == targets[:, None]
    local_target = jnp.sum(jnp.where(matches, logits, jnp.zeros_like(logits)), axis=1)
    owned_peak = jnp.max(logits, axis=1)
    local_expsum = jnp.sum(jnp.exp(logits - owned_peak[:, None]), axis=1)
    peak_logit, expsum, target_logit = joined_all(
        (owned_peak, local_expsum, local_target), FSDP_TENSOR, combine_stats
    )
    logprob = target_logit - peak_logit - jnp.log(expsum)
    greedy_gap = target_logit - peak_logit
    return (logprob, greedy_gap)


def solution(mesh):
    torus = Mesh(
        mesh.devices.reshape(8, 4, 2, 2, 4), ("fsdp_0", "fsdp_1", "fsdp_2", "tensor_0", "tensor_1")
    )
    placed = (P(None, FSDP), P(TENSOR, FSDP), P())
    return jax.shard_map(
        per_device, mesh=torus, in_specs=placed, out_specs=(P(), P()), check_vma=False
    )
```

profile of v0, /device:TPU:1, one launch (start us, length us, event | category | flops | bytes accessed | tf_op | source)
XLA Modules:
  0.0 200.6 jit_solution(8799917515166575782)
XLA Ops:
  7.2 0.0 all-gather.12.cloned.1.call-start
  7.2 0.7 all-gather.12.cloned.1.call-update
  7.9 17.6 %all-to-all-start = ((bf16[64,128,128]{2,1,0:T(8,128)(2,1)}), bf16[64,128,128]{2,1,0:T(8,128)(2,1)S(1)}, u32[]{:S(2)}, u32[]{:S(2)}) async-start(bf16[64,128,128]{2,1,0:T(8,128)(2,1)} %bitcast.317), calls=%async_computation | async-start | bytes 4194304 | tf_op jit(solution)/shard_map/all_to_all | solution.py:54
  25.6 69.0 %all-to-all-done = bf16[64,128,128]{2,1,0:T(8,128)(2,1)S(1)} async-done(((bf16[64,128,128]{2,1,0:T(8,128)(2,1)}), bf16[64,128,128]{2,1,0:T(8,128)(2,1)S(1)}, u32[]{:S(2)}, u32[]{:S(2)}) %all-to-all-start) | async-done | bytes 2097184 | tf_op jit(solution)/shard_map/all_to_all | solution.py:54
  94.6 2.9 %copy.6 = bf16[128,64,128]{0,2,1:T(8,128)(2,1)} copy(bf16[128,64,128]{2,0,1:T(8,128)(2,1)S(1)} %bitcast.315) | data formatting | bytes 4194304 | tf_op jit(solution)/shard_map/all_to_all | solution.py:54
  97.5 38.1 %all-gather.12.cloned.1.call-done = bf16[256,8192]{1,0:T(8,128)(2,1)} async-done(((bf16[256,128]{1,0:T(8,128)(2,1)}), bf16[256,8192]{1,0:T(8,128)(2,1)}) %all-gather.12.cloned.1.call-update) | async-done | bytes 4194320 | tf_op jit(solution)/shard_map/all_gather | solution.py:57
  135.6 0.0 copy-start
  135.6 4.4 %fusion.56 = (f32[256]{0:T(256)S(1)}, f32[256,128]{0,1:T(8,128)S(1)}) fusion(bf16[256,8192]{1,0:T(8,128)(2,1)} %all-gather.12.cloned.1.call-done, bf16[128,8192]{0,1:T(8,128)(2,1)} %bitcast.316), kind=kOutput, calls=%fused_computation.109 | convolution fusion | flops 536903424 | bytes 6423552 | tf_op jit(solution)/shard_map/dot_general | solution.py:39
  140.0 0.0 copy-done
  140.0 0.1 exponential_reduce_fusion
  140.1 18.3 %all-gather.5 = f32[8,3,256]{2,1,0:T(4,128)S(1)} all-gather(f32[1,3,256]{2,1,0:T(4,128)S(1)} %maximum_bitcast_fusion), channel_id=2, replica_groups=mesh['fsdp_0'=8,'fsdp_1'=4,'fsdp_2'=2,'tensor_0'=2,'tensor_1'=4] {'fsdp_0'}, dimensions={0}, use_global_device_ids=true | all-gather | bytes 27648 | tf_op jit(solution)/shard_map/all_gather | solution.py:20
  158.5 10.9 %all-gather.6 = f32[4,3,256]{2,1,0:T(4,128)S(1)} all-gather(f32[1,3,256]{2,1,0:T(4,128)S(1)} %maximum_bitcast_fusion.1), channel_id=3, replica_groups=mesh['fsdp_0'=8,'fsdp_1'=4,'fsdp_2'=2,'tensor_0'=2,'tensor_1'=4] {'fsdp_1'}, dimensions={0}, use_global_device_ids=true | all-gather | bytes 15360 | tf_op jit(solution)/shard_map/all_gather | solution.py:20
  169.5 11.0 %all-gather.7 = f32[2,3,256]{2,1,0:T(4,128)S(1)} all-gather(f32[1,3,256]{2,1,0:T(4,128)S(1)} %maximum_bitcast_fusion.2), channel_id=4, replica_groups=mesh['fsdp_0'=8,'fsdp_1'=4,'fsdp_2'=2,'tensor_0'=2,'tensor_1'=4] {'fsdp_2'}, dimensions={0}, use_global_device_ids=true | all-gather | bytes 9216 | tf_op jit(solution)/shard_map/all_gather | solution.py:20
  180.5 3.2 %all-gather.8 = f32[2,3,256]{2,1,0:T(4,128)S(1)} all-gather(f32[1,3,256]{2,1,0:T(4,128)S(1)} %maximum_bitcast_fusion.3), channel_id=5, replica_groups=mesh['fsdp_0'=8,'fsdp_1'=4,'fsdp_2'=2,'tensor_0'=2,'tensor_1'=4] {'tenso..., dimensions={0}, use_global_device_ids=true | all-gather | bytes 9216 | tf_op jit(solution)/shard_map/all_gather | solution.py:20
  183.7 9.4 %all-gather.9 = f32[4,3,256]{2,1,0:T(4,128)S(1)} all-gather(f32[1,3,256]{2,1,0:T(4,128)S(1)} %maximum_bitcast_fusion.4), channel_id=6, replica_groups=mesh['fsdp_0'=8,'fsdp_1'=4,'fsdp_2'=2,'tensor_0'=2,'tensor_1'=4] {'tenso..., dimensions={0}, use_global_device_ids=true | all-gather | bytes 15360 | tf_op jit(solution)/shard_map/all_gather | solution.py:20
  193.2 0.6 log_subtract_fusion
  (15 shorter events, 0.2 us)
Async XLA Ops:
  7.2 128.4 %all-gather.12.cloned.1.call-start = ((), (), s32[]{:S(2)}) async-start(), calls=%async_computation.1 | async-start | bytes 4259840 | tf_op jit(solution)/shard_map/all_gather | solution.py:57
  7.9 86.7 %all-to-all-start = ((bf16[64,128,128]{2,1,0:T(8,128)(2,1)}), bf16[64,128,128]{2,1,0:T(8,128)(2,1)S(1)}, u32[]{:S(2)}, u32[]{:S(2)}) async-start(bf16[64,128,128]{2,1,0:T(8,128)(2,1)} %bitcast.317), calls=%async_computation | async-start | bytes 4194304 | tf_op jit(solution)/shard_map/all_to_all | solution.py:54
  135.6 4.4 %copy-start = (s32[256]{0:T(256)S(1)}, s32[256]{0:T(256)}, u32[]{:S(2)}) copy-start(s32[256]{0:T(256)} %param.5) | copy-start | bytes 3076
Sparse Core Ops, SparseCore 0:
  11.2 124.3 all-gather.11
where the time goes:
time: 203 us; the launch traced here: 201 us
  waiting for transfers between devices  108 us (53%)
  blocking collectives  52.8 us (26%)
  starting transfers between devices  17.7 us (9%)
  between operations  14.1 us (7%)
  matrix products  4.39 us (2%)
  local copies, waits for them, and re-layouts  2.91 us (1%)
    all_to_all x1, waiting for transfers between devices, per_device(): lax.all_to_all(head_weight, FSDP, split_axis=0, concat_axis=1, tiled=True)  69 us
    all_gather x5, blocking collectives, all_in_one(): both, at, found = (lax.all_gather(jnp.concatenate(lines), axis), 0, {})  52.8 us
    all_gather x1, waiting for transfers between devices, per_device(): gathered = lax.all_gather(hidden, FSDP, axis=1, tiled=True)  38.1 us
    all_to_all x1, starting transfers between devices, per_device(): lax.all_to_all(head_weight, FSDP, split_axis=0, concat_axis=1, tiled=True)  17.6 us
    dot_general x1, matrix products, contract_rows(): lax.dot_general(left, right, (((1,), (1,)), ((), ())), preferred_element_...  4.39 us
  transfers between devices with their start and end apart: 2, of which 2 were waited for; matrix products, arithmetic and copies ran while one was open for 1% of the time, Pallas kernels for 0%

commit v1 on v0

v1 whole, which is shorter than its diff:
```python
import jax
import jax.numpy as jnp
from jax import lax
from jax.experimental import pallas as pl
from jax.experimental.pallas import tpu as pltpu
from jax.sharding import Mesh
from jax.sharding import PartitionSpec as P

Z, Y, CORE, YL, X = "fsdp_0", "fsdp_1", "fsdp_2", "tensor_0", "tensor_1"
FSDP = (Z, Y, CORE)
TENSOR = (YL, X)
OWNERS = (Z, Y)
FIRST = (Z, CORE)
SECOND = (Y, YL, X)
LANES = 128


def encode(value):
    square = value * jnp.abs(value)
    return (square * jnp.abs(square)).astype(jnp.bfloat16)


def decode(code):
    code = code.astype(jnp.float32)
    root = lax.rsqrt(lax.rsqrt(jnp.abs(code)))
    return jnp.where(code < 0, -root, root)


def partial_kernel(_, own_ref, their_ref, own_hidden_ref, their_hidden_ref, out_ref):
    rows = jnp.concatenate([own_ref[...], their_ref[...]], axis=1)
    hidden = jnp.concatenate([own_hidden_ref[...], their_hidden_ref[...]], axis=1)
    logits = lax.dot_general(
        rows, hidden, (((1,), (1,)), ((), ())), preferred_element_type=jnp.float32
    )
    out_ref[...] = encode(logits)


def partial_logits(core, head_weight, hidden, swapped):
    half = head_weight.shape[0] // 2
    tokens, depth = hidden.shape
    block = min(512, half)
    steps = half // block
    return pl.pallas_call(
        partial_kernel,
        grid_spec=pltpu.PrefetchScalarGridSpec(
            num_scalar_prefetch=1,
            grid=(steps,),
            in_specs=[
                pl.BlockSpec((block, depth), lambda i, c: (c[0] * steps + i, 0)),
                pl.BlockSpec((block, depth), lambda i, c: (i, 0)),
                pl.BlockSpec((tokens, depth), lambda i, c: (0, 0)),
                pl.BlockSpec((tokens, depth), lambda i, c: (half // tokens, 0)),
            ],
            out_specs=pl.BlockSpec((block, tokens), lambda i, c: (i, 0)),
        ),
        out_shape=jax.ShapeDtypeStruct((half, tokens), jnp.bfloat16),
        name="partial_logits",
    )(core, head_weight, swapped, hidden, swapped)


def put_stats(out_ref, peak, expsum, target):
    zeros = jnp.zeros((2, LANES), jnp.float32)
    packed = jnp.concatenate([peak, expsum, target, zeros], axis=0)
    for k in range(out_ref.shape[0]):
        out_ref[k] = packed


def two_rows(row):
    return jnp.concatenate([row[:, :LANES], row[:, LANES:]], axis=0)


def stats_kernel(codes_ref, target_ref, out_ref, logits_ref):
    peers, rows, tokens = codes_ref.shape
    step = 32

    def add_rows(k, peak):
        at = pl.ds(pl.multiple_of(k * step, step), step)
        total = decode(codes_ref[0, at, :])
        for peer in range(1, peers):
            total = total + decode(codes_ref[peer, at, :])
        logits_ref[at, :] = total
        return jnp.maximum(peak, jnp.max(total, axis=0, keepdims=True))

    peak = lax.fori_loop(
        0, rows // step, add_rows, jnp.full((1, tokens), -jnp.inf, jnp.float32)
    )
    expsum = jnp.sum(jnp.exp(logits_ref[...] - peak), axis=0, keepdims=True)
    put_stats(out_ref, two_rows(peak), two_rows(expsum), target_ref[...])


def combine(parts):
    peaks, expsums, targets = parts[:, 0:2], parts[:, 2:4], parts[:, 4:6]
    peak = jnp.max(peaks, axis=0)
    expsum = jnp.sum(expsums * jnp.exp(peaks - peak), axis=0)
    return peak, expsum, jnp.sum(targets, axis=0)


def combine_kernel(parts_ref, out_ref):
    put_stats(out_ref, *combine(parts_ref[...]))


def finish_kernel(parts_ref, logprob_ref, gap_ref):
    peak, expsum, target = combine(parts_ref[...])
    logprob_ref[...] = target - peak - jnp.log(expsum)
    gap_ref[...] = target - peak


def own_target(hidden, head_weight, targets):
    held = head_weight.shape[0]
    local = targets - lax.axis_index(TENSOR) * held
    rows = jnp.take(head_weight, jnp.clip(local, 0, held - 1), axis=0)
    share = jnp.sum(rows.astype(jnp.float32) * hidden.astype(jnp.float32), axis=1)
    return jnp.where((local >= 0) & (local < held), share, 0.0)


def per_device(hidden, head_weight, targets):
    held = head_weight.shape[0]
    tokens = hidden.shape[0]
    half = held // 2
    core = lax.axis_index(CORE)
    others = lax.dynamic_slice_in_dim(head_weight, (1 - core) * half, half, axis=0)
    swapped = lax.ppermute(jnp.concatenate([others, hidden]), CORE, [(0, 1), (1, 0)])
    codes = partial_logits(core.reshape(1).astype(jnp.int32), head_weight, hidden, swapped)
    peers = lax.axis_size(OWNERS)
    codes = lax.all_to_all(codes.reshape(peers, half // peers, tokens), OWNERS, 0, 0)
    target = own_target(hidden, head_weight, targets).reshape(2, LANES)
    stats = pl.pallas_call(
        stats_kernel,
        out_shape=jax.ShapeDtypeStruct((lax.axis_size(FIRST), 8, LANES), jnp.float32),
        scratch_shapes=[pltpu.VMEM((half // peers, tokens), jnp.float32)],
        name="stats",
    )(codes, target)
    stats = lax.all_to_all(stats, FIRST, 0, 0)
    stats = pl.pallas_call(
        combine_kernel,
        out_shape=jax.ShapeDtypeStruct((lax.axis_size(SECOND), 8, LANES), jnp.float32),
        name="combine",
    )(stats)
    stats = lax.all_to_all(stats, SECOND, 0, 0)
    pair = jax.ShapeDtypeStruct((2, LANES), jnp.float32)
    logprob, gap = pl.pallas_call(finish_kernel, out_shape=(pair, pair), name="finish")(stats)
    return logprob.reshape(tokens), gap.reshape(tokens)


def solution(mesh):
    torus = Mesh(mesh.devices.reshape(8, 4, 2, 2, 4), FSDP + TENSOR)
    placed = (P(None, FSDP), P(TENSOR, FSDP), P())
    return jax.shard_map(
        per_device, mesh=torus, in_specs=placed, out_specs=(P(), P()), check_vma=False
    )
```

time: 203 us -> 134 us (0.66); the launches traced: 201 us -> 134 us
  waiting for transfers between devices: 108 us -> 60.1 us
  blocking collectives: 52.8 us -> 33.2 us
  between operations: 14.1 us -> 0.72 us
  Pallas kernels: 0 us -> 13.3 us
  matrix products: 4.39 us -> 0 us
  local copies, waits for them, and re-layouts: 2.91 us -> 6.29 us
    all_gather x5 -> x0, blocking collectives: 52.8 us -> none  [all_in_one(): both, at, found = (lax.all_gather(jnp.concatenate(lines), axis), 0, {})]
    all_gather x1 -> x0, waiting for transfers between devices: 38.1 us -> none  [per_device(): gathered = lax.all_gather(hidden, FSDP, axis=1, tiled=True)]
    all_to_all x0 -> x2, blocking collectives: none -> 33.2 us  [the longest x1 18.8 us: per_device(): stats = lax.all_to_all(stats, FIRST, 0, 0)]
    pallas_call x0 -> x4, Pallas kernels: none -> 13.3 us  [the longest x1 6.72 us: partial_logits(): pl.pallas_call(partial_kernel, grid_spec=pltpu.PrefetchScalarGridSpec(num...]
    all_to_all x1, waiting for transfers between devices: 69 us -> 57.8 us  [per_device(): lax.all_to_all(codes.reshape(peers, half // peers, tokens), OWNERS, 0, 0)]
    ppermute x0 -> x1, starting transfers between devices: none -> 8.75 us  [per_device(): lax.ppermute(jnp.concatenate([others, hidden]), CORE, [(0, 1), (1, 0)])]
    all_to_all x1, starting transfers between devices: 17.6 us -> 10.5 us  [per_device(): lax.all_to_all(codes.reshape(peers, half // peers, tokens), OWNERS, 0, 0)]
    dot_general x1 -> x0, matrix products: 4.39 us -> none  [contract_rows(): lax.dot_general(left, right, (((1,), (1,)), ((), ())), preferred_element_...]
  transfers between devices with their start and end apart: 2 -> 2, of which waited for: 2 -> 2; matrix products, arithmetic and copies ran while one was open for 1% -> 3% of each run, Pallas kernels for 0% -> 0%
where the time goes in v1:
time: 134 us
  waiting for transfers between devices  60.1 us (45%)
  blocking collectives  33.2 us (25%)
  starting transfers between devices  19.2 us (14%)
  Pallas kernels  13.3 us (10%)
  local copies, waits for them, and re-layouts  6.29 us (5%)
    all_to_all x1, waiting for transfers between devices, per_device(): lax.all_to_all(codes.reshape(peers, half // peers, tokens), OWNERS, 0, 0)  57.8 us
    all_to_all x1, blocking collectives, per_device(): stats = lax.all_to_all(stats, FIRST, 0, 0)  18.8 us
    all_to_all x1, blocking collectives, per_device(): stats = lax.all_to_all(stats, SECOND, 0, 0)  14.4 us
    all_to_all x1, starting transfers between devices, per_device(): lax.all_to_all(codes.reshape(peers, half // peers, tokens), OWNERS, 0, 0)  10.5 us
    ppermute x1, starting transfers between devices, per_device(): lax.ppermute(jnp.concatenate([others, hidden]), CORE, [(0, 1), (1, 0)])  8.75 us
    pallas_call x1, Pallas kernels, partial_logits(): pl.pallas_call(partial_kernel, grid_spec=pltpu.PrefetchScalarGridSpec(num...  6.72 us
    pallas_call x1, Pallas kernels, per_device(): pl.pallas_call(stats_kernel, out_shape=jax.ShapeDtypeStruct((lax.axis_siz...  3.48 us
  transfers between devices with their start and end apart: 2, of which 2 were waited for; matrix products, arithmetic and copies ran while one was open for 3% of the time, Pallas kernels for 0%

profile of v1, /device:TPU:1, one launch (start us, length us, event | category | flops | bytes accessed | tf_op | source)
XLA Modules:
  0.0 133.7 jit_solution(9077674565463294414)
XLA Ops:
  0.6 0.0 copy-start.2
  0.6 1.3 constant_dynamic-slice_fusion
  2.0 0.0 copy-done.2
  2.0 0.1 pad_maximum_fusion
  2.1 8.7 %collective-permute-start = (bf16[4352,128]{1,0:T(8,128)(2,1)S(1)}, bf16[4352,128]{1,0:T(8,128)(2,1)S(1)}, u32[]{:S(2)}, u32[]{:S(2)}) collective-permute-start(bf16[4352,128]{1,0:T(8,128)(2,1)S(1)} %pad_maximum_fusion), channel_id=1, source_target_pairs={{0,8},{8,0},{1,9},{9,1},{2,10},{10,2},{3,11},{11,3},{4,12},{12,4},... | collective-permute-start | bytes 3342344 | tf_op jit(solution)/shard_map/ppermute | solution.py:122
  10.8 2.4 %collective-permute-done.their_ref.their_hidden_ref = bf16[4352,128]{1,0:T(8,128)(2,1)S(1)} collective-permute-done((bf16[4352,128]{1,0:T(8,128)(2,1)S(1)}, bf16[4352,128]{1,0:T(8,128)(2,1)S(1)}, u32[]{:S(2)}, u32[]{:S(2)}) %collective-permute-start) | collective-permute-done | bytes 1114144 | tf_op jit(solution)/shard_map/ppermute | solution.py:122
  13.2 0.0 copy-start.1
  13.2 1.0 copy-done.1
  14.2 6.7 %partial_logits.1 = bf16[4096,256]{1,0:T(8,128)(2,1)} custom-call(s32[1]{0:T(128)} %bitcast._, bf16[8192,128]{1,0:T(8,128)(2,1)} %own_ref.1, bf16[4352,128]{1,0:T(8,128)(2,1)} %copy-done.1, bf16[256,128]{1,0:T(8,128)(2,1)} %own_hidden_ref.1, bf16[4352,128]{1,0:T(8,128)(2,1)} %copy-done.1), custom_call_target="tpu_custom_call" | custom-call | tf_op jit(solution)/shard_map/partial_logits/pallas_call | solution.py:43
  20.9 0.0 copy-start.4
  20.9 0.0 copy-start.3
  20.9 10.5 %all-to-all-start = ((bf16[32,128,256]{2,1,0:T(8,128)(2,1)}), bf16[32,128,256]{2,1,0:T(8,128)(2,1)S(1)}, u32[]{:S(2)}, u32[]{:S(2)}) async-start(bf16[32,128,256]{2,1,0:T(8,128)(2,1)} %bitcast.6), calls=%async_computation | async-start | bytes 4194304 | tf_op jit(solution)/shard_map/all_to_all | solution.py:125
  31.4 0.0 copy-done.4
  31.5 2.6 %gather_fusion = bf16[256,128]{1,0:T(8,128)(2,1)S(1)} fusion(bf16[8192,128]{1,0:T(8,128)(2,1)} %own_ref.1, s32[1024]{0:T(1024)S(1)} %pad_clamp_fusion), kind=kCustom, calls=%fused_computation | custom fusion | bytes 132096 | tf_op jit(solution)/shard_map/jit(_take)/gather | solution.py:111
  34.0 0.0 copy-done.3
  34.0 0.2 multiply_reduce_fusion
  34.2 0.6 fusion.target_ref
  34.8 57.8 %all-to-all-done.codes_ref = bf16[32,128,256]{2,1,0:T(8,128)(2,1)S(1)} async-done(((bf16[32,128,256]{2,1,0:T(8,128)(2,1)}), bf16[32,128,256]{2,1,0:T(8,128)(2,1)S(1)}, u32[]{:S(2)}, u32[]{:S(2)}) %all-to-all-start) | async-done | bytes 2097184 | tf_op jit(solution)/shard_map/all_to_all | solution.py:125
  92.6 1.3 %copy-done = bf16[32,128,256]{2,1,0:T(8,128)(2,1)} copy-done((bf16[32,128,256]{2,1,0:T(8,128)(2,1)}, bf16[32,128,256]{2,1,0:T(8,128)(2,1)S(1)}, u32[]{:S(2)}) %copy-start) | copy-done | bytes 2097176
  93.9 3.5 %stats.1 = f32[16,8,128]{2,1,0:T(8,128)} custom-call(bf16[32,128,256]{2,1,0:T(8,128)(2,1)} %copy-done, f32[2,128]{1,0:T(2,128)} %fusion.target_ref), custom_call_target="tpu_custom_call" | custom-call | tf_op jit(solution)/shard_map/stats/pallas_call | solution.py:127
  97.4 18.8 %all_to_all.15.parts_ref = f32[16,8,128]{2,1,0:T(8,128)} all-to-all(f32[16,8,128]{2,1,0:T(8,128)} %stats.1), channel_id=1, replica_groups=mesh['fsdp_0'=8,'fsdp_1'=4,'fsdp_2'=2,'tensor_0'=2,'tensor_1'=4] {'fsdp_..., dimensions={0} | all-to-all | bytes 131072 | tf_op jit(solution)/shard_map/all_to_all | solution.py:133
  116.2 1.5 %combine.1 = f32[32,8,128]{2,1,0:T(8,128)} custom-call(f32[16,8,128]{2,1,0:T(8,128)} %all_to_all.15.parts_ref), custom_call_target="tpu_custom_call" | custom-call | tf_op jit(solution)/shard_map/combine/pallas_call | solution.py:134
  117.8 14.4 %all_to_all.16.parts_ref = f32[32,8,128]{2,1,0:T(8,128)} all-to-all(f32[32,8,128]{2,1,0:T(8,128)} %combine.1), channel_id=1, replica_groups=mesh['fsdp_0'=8,'fsdp_1'=4,'fsdp_2'=2,'tensor_0'=2,'tensor_1'=4] {'fsdp_..., dimensions={0} | all-to-all | bytes 262144 | tf_op jit(solution)/shard_map/all_to_all | solution.py:139
  132.1 1.5 %finish.1 = (f32[2,128]{1,0:T(2,128)}, f32[2,128]{1,0:T(2,128)}) custom-call(f32[32,8,128]{2,1,0:T(8,128)} %all_to_all.16.parts_ref), custom_call_target="tpu_custom_call" | custom-call | tf_op jit(solution)/shard_map/finish/pallas_call | solution.py:141
  (3 shorter events, 0.0 us)
Async XLA Ops:
  0.6 1.4 %copy-start.2 = (bf16[256,128]{1,0:T(8,128)(2,1)S(1)}, bf16[256,128]{1,0:T(8,128)(2,1)}, u32[]{:S(2)}) copy-start(bf16[256,128]{1,0:T(8,128)(2,1)} %own_hidden_ref.1) | copy-start | bytes 196612
  2.1 11.1 %collective-permute-start = (bf16[4352,128]{1,0:T(8,128)(2,1)S(1)}, bf16[4352,128]{1,0:T(8,128)(2,1)S(1)}, u32[]{:S(2)}, u32[]{:S(2)}) collective-permute-start(bf16[4352,128]{1,0:T(8,128)(2,1)S(1)} %pad_maximum_fusion), channel_id=1, source_target_pairs={{0,8},{8,0},{1,9},{9,1},{2,10},{10,2},{3,11},{11,3},{4,12},{12,4},... | collective-permute-start | bytes 3342344 | tf_op jit(solution)/shard_map/ppermute | solution.py:122
  13.2 1.0 copy-start.1
  20.9 10.5 %copy-start.4 = (s32[256]{0:T(256)S(1)}, s32[256]{0:T(256)}, u32[]{:S(2)}) copy-start(s32[256]{0:T(256)} %param.5) | copy-start | bytes 3076
  20.9 13.1 %copy-start.3 = (bf16[256,128]{1,0:T(8,128)(2,1)S(1)}, bf16[256,128]{1,0:T(8,128)(2,1)}, u32[]{:S(2)}) copy-start(bf16[256,128]{1,0:T(8,128)(2,1)} %own_hidden_ref.1) | copy-start | bytes 196612
  20.9 71.7 %all-to-all-start = ((bf16[32,128,256]{2,1,0:T(8,128)(2,1)}), bf16[32,128,256]{2,1,0:T(8,128)(2,1)S(1)}, u32[]{:S(2)}, u32[]{:S(2)}) async-start(bf16[32,128,256]{2,1,0:T(8,128)(2,1)} %bitcast.6), calls=%async_computation | async-start | bytes 4194304 | tf_op jit(solution)/shard_map/all_to_all | solution.py:125
  92.6 1.3 %copy-start = (bf16[32,128,256]{2,1,0:T(8,128)(2,1)}, bf16[32,128,256]{2,1,0:T(8,128)(2,1)S(1)}, u32[]{:S(2)}) copy-start(bf16[32,128,256]{2,1,0:T(8,128)(2,1)S(1)} %all-to-all-done.codes_ref) | copy-start | bytes 6291460

commit v2 on v1

--- a/solution.py
+++ b/solution.py
@@ -26,36 +26,32 @@
     return jnp.where(code < 0, -root, root)
 
 
-def partial_kernel(_, own_ref, their_ref, own_hidden_ref, their_hidden_ref, out_ref):
-    rows = jnp.concatenate([own_ref[...], their_ref[...]], axis=1)
-    hidden = jnp.concatenate([own_hidden_ref[...], their_hidden_ref[...]], axis=1)
-    logits = lax.dot_general(
-        rows, hidden, (((1,), (1,)), ((), ())), preferred_element_type=jnp.float32
-    )
-    out_ref[...] = encode(logits)
+def partial_kernel(own_ref, swapped_ref, hidden_ref, out_ref):
+    half, depth = own_ref.shape
+    tokens = hidden_ref.shape[0]
+    hidden = jnp.concatenate([hidden_ref[...], swapped_ref[half : half + tokens, :]], axis=1)
+    step = min(512, half)
+
+    def add_rows(k, carry):
+        at = pl.ds(pl.multiple_of(k * step, step), step)
+        rows = jnp.concatenate([own_ref[at, :], swapped_ref[at, :]], axis=1)
+        logits = lax.dot_general(
+            rows, hidden, (((1,), (1,)), ((), ())), preferred_element_type=jnp.float32
+        )
+        out_ref[at, :] = encode(logits)
+        return carry
+
+    lax.fori_loop(0, half // step, add_rows, 0)
 
 
-def partial_logits(core, head_weight, hidden, swapped):
-    half = head_weight.shape[0] // 2
-    tokens, depth = hidden.shape
-    block = min(512, half)
-    steps = half // block
+def local_call(kernel, name, out, *operands, place=pltpu.VMEM, **more):
+    results = [place(shape, dtype) for shape, dtype in out]
+    specs = [pl.BlockSpec(memory_space=pltpu.VMEM)] * len(operands)
+    operands = [pltpu.with_memory_space_constraint(x, pltpu.VMEM) for x in operands]
+    params = pltpu.CompilerParams(vmem_limit_bytes=16 * 2**20)
     return pl.pallas_call(
-        partial_kernel,
-        grid_spec=pltpu.PrefetchScalarGridSpec(
-            num_scalar_prefetch=1,
-            grid=(steps,),
-            in_specs=[
-                pl.BlockSpec((block, depth), lambda i, c: (c[0] * steps + i, 0)),
-                pl.BlockSpec((block, depth), lambda i, c: (i, 0)),
-                pl.BlockSpec((tokens, depth), lambda i, c: (0, 0)),
-                pl.BlockSpec((tokens, depth), lambda i, c: (half // tokens, 0)),
-            ],
-            out_specs=pl.BlockSpec((block, tokens), lambda i, c: (i, 0)),
-        ),
-        out_shape=jax.ShapeDtypeStruct((half, tokens), jnp.bfloat16),
-        name="partial_logits",
-    )(core, head_weight, swapped, hidden, swapped)
+        kernel, in_specs=specs, out_shape=results, name=name, compiler_params=params, **more
+    )(*operands)
 
 
 def put_stats(out_ref, peak, expsum, target):
@@ -117,28 +113,37 @@
     held = head_weight.shape[0]
     tokens = hidden.shape[0]
     half = held // 2
+    peers = lax.axis_size(OWNERS)
     core = lax.axis_index(CORE)
     others = lax.dynamic_slice_in_dim(head_weight, (1 - core) * half, half, axis=0)
+    own = lax.dynamic_slice_in_dim(head_weight, core * half, half, axis=0)
     swapped = lax.ppermute(jnp.concatenate([others, hidden]), CORE, [(0, 1), (1, 0)])
-    codes = partial_logits(core.reshape(1).astype(jnp.int32), head_weight, hidden, swapped)
-    peers = lax.axis_size(OWNERS)
+    (codes,) = local_call(
+        partial_kernel, "partial", [((half, tokens), jnp.bfloat16)], own, swapped, hidden
+    )
+    target = own_target(hidden, head_weight, targets).reshape(2, LANES)
+    codes, target = lax.optimization_barrier((codes, target))
     codes = lax.all_to_all(codes.reshape(peers, half // peers, tokens), OWNERS, 0, 0)
-    target = own_target(hidden, head_weight, targets).reshape(2, LANES)
-    stats = pl.pallas_call(
+    (stats,) = local_call(
         stats_kernel,
-        out_shape=jax.ShapeDtypeStruct((lax.axis_size(FIRST), 8, LANES), jnp.float32),
+        "stats",
+        [((lax.axis_size(FIRST), 8, LANES), jnp.float32)],
+        codes,
+        target,
         scratch_shapes=[pltpu.VMEM((half // peers, tokens), jnp.float32)],
-        name="stats",
-    )(codes, target)
+    )
     stats = lax.all_to_all(stats, FIRST, 0, 0)
-    stats = pl.pallas_call(
-        combine_kernel,
-        out_shape=jax.ShapeDtypeStruct((lax.axis_size(SECOND), 8, LANES), jnp.float32),
-        name="combine",
-    )(stats)
+    (stats,) = local_call(
+        combine_kernel, "combine", [((lax.axis_size(SECOND), 8, LANES), jnp.float32)], stats
+    )
     stats = lax.all_to_all(stats, SECOND, 0, 0)
-    pair = jax.ShapeDtypeStruct((2, LANES), jnp.float32)
-    logprob, gap = pl.pallas_call(finish_kernel, out_shape=(pair, pair), name="finish")(stats)
+    logprob, gap = local_call(
+        finish_kernel,
+        "finish",
+        [((2, LANES), jnp.float32)] * 2,
+        stats,
+        place=jax.ShapeDtypeStruct,
+    )
     return logprob.reshape(tokens), gap.reshape(tokens)
 
 

time: 134 us -> 121 us (0.903)
  blocking collectives: 33.2 us -> 103 us
  waiting for transfers between devices: 60.1 us -> 0.01 us
  starting transfers between devices: 19.2 us -> 8.75 us
  Pallas kernels: 13.3 us -> 4.18 us
  local copies, waits for them, and re-layouts: 6.29 us -> 4.32 us
    all_to_all x0 -> x1, blocking collectives: none -> 73.4 us  [per_device(): lax.all_to_all(codes.reshape(peers, half // peers, tokens), OWNERS, 0, 0)]
    all_to_all x1 -> x0, waiting for transfers between devices: 57.8 us -> none  [per_device(): lax.all_to_all(codes.reshape(peers, half // peers, tokens), OWNERS, 0, 0)]
    all_to_all x1 -> x0, starting transfers between devices: 10.5 us -> none  [per_device(): lax.all_to_all(codes.reshape(peers, half // peers, tokens), OWNERS, 0, 0)]
    pallas_call x4, Pallas kernels: 13.3 us -> 4.18 us  [local_call(): pl.pallas_call(kernel, in_specs=specs, out_shape=results, name=name, comp...]
    all_to_all x1, blocking collectives: 18.8 us -> 11.8 us  [per_device(): stats = lax.all_to_all(stats, FIRST, 0, 0)]
    all_to_all x1, blocking collectives: 14.4 us -> 17.8 us  [per_device(): stats = lax.all_to_all(stats, SECOND, 0, 0)]
    ppermute x1, waiting for transfers between devices: 2.36 us -> 0.01 us  [per_device(): lax.ppermute(jnp.concatenate([others, hidden]), CORE, [(0, 1), (1, 0)])]
    unnamed x10 -> x4, local copies, waits for them, and re-layouts: 2.37 us -> 0.01 us
  transfers between devices with their start and end apart: 2 -> 1, of which waited for: 2 -> 0; matrix products, arithmetic and copies ran while one was open for 3% -> 2% of each run, Pallas kernels for 0% -> 0%
where the time goes in v2:
time: 121 us
  blocking collectives  103 us (85%)
  starting transfers between devices  8.75 us (7%)
  local copies, waits for them, and re-layouts  4.32 us (4%)
  Pallas kernels  4.18 us (3%)
    all_to_all x1, blocking collectives, per_device(): lax.all_to_all(codes.reshape(peers, half // peers, tokens), OWNERS, 0, 0)  73.4 us
    all_to_all x1, blocking collectives, per_device(): stats = lax.all_to_all(stats, SECOND, 0, 0)  17.8 us
    all_to_all x1, blocking collectives, per_device(): stats = lax.all_to_all(stats, FIRST, 0, 0)  11.8 us
    ppermute x1, starting transfers between devices, per_device(): lax.ppermute(jnp.concatenate([others, hidden]), CORE, [(0, 1), (1, 0)])  8.75 us
    pallas_call x4, Pallas kernels, local_call(): pl.pallas_call(kernel, in_specs=specs, out_shape=results, name=name, comp...  4.18 us
    gather x1, local copies, waits for them, and re-layouts, own_target(): rows = jnp.take(head_weight, jnp.clip(local, 0, held - 1), axis=0)  2.59 us
  transfers between devices with their start and end apart: 1, of which 0 were waited for; matrix products, arithmetic and copies ran while one was open for 2% of the time, Pallas kernels for 0%

profile of v2, /device:TPU:1, one launch (start us, length us, event | category | flops | bytes accessed | tf_op | source)
XLA Modules:
  0.0 121.3 jit_solution(1915693536507740171)
XLA Ops:
  0.6 0.0 copy-start
  0.6 1.7 %constant_dynamic-slice_fusion = (bf16[4096,128]{1,0:T(8,128)(2,1)S(1)}, bf16[4096,128]{1,0:T(8,128)(2,1)S(1)}) fusion(bf16[8192,128]{1,0:T(8,128)(2,1)} %param.4, s32[]{:T(128)S(6)} %select_n.20, s32[]{:T(128)S(6)} %select_n.19), kind=kLoop, calls=%fused_computation.8 | loop fusion | bytes 4194312 | tf_op jit(solution)/shard_map/dynamic_slice | solution.py:118
  2.4 0.0 copy-start.1
  2.4 0.0 copy-done
  2.4 0.1 pad_maximum_fusion
  2.5 8.7 %collective-permute-start = (bf16[4352,128]{1,0:T(8,128)(2,1)S(1)}, bf16[4352,128]{1,0:T(8,128)(2,1)S(1)}, u32[]{:S(2)}, u32[]{:S(2)}) collective-permute-start(bf16[4352,128]{1,0:T(8,128)(2,1)S(1)} %pad_maximum_fusion), channel_id=1, source_target_pairs={{0,8},{8,0},{1,9},{9,1},{2,10},{10,2},{3,11},{11,3},{4,12},{12,4},... | collective-permute-start | bytes 3342344 | tf_op jit(solution)/shard_map/ppermute | solution.py:120
  11.2 0.0 copy-done.1
  11.3 2.6 %gather_fusion = bf16[256,128]{1,0:T(8,128)(2,1)S(1)} fusion(bf16[8192,128]{1,0:T(8,128)(2,1)} %param.4, s32[1024]{0:T(1024)S(1)} %pad_clamp_fusion), kind=kCustom, calls=%fused_computation | custom fusion | bytes 132096 | tf_op jit(solution)/shard_map/jit(_take)/gather | solution.py:107
  13.9 0.2 multiply_reduce_fusion
  14.1 0.0 collective-permute-done.swapped_ref
  14.1 2.2 %partial.1 = bf16[4096,256]{1,0:T(8,128)(2,1)S(1)} custom-call(bf16[4096,128]{1,0:T(8,128)(2,1)S(1)} %get-tuple-element.13.own_ref, bf16[4352,128]{1,0:T(8,128)(2,1)S(1)} %collective-permute-done.swapped_ref, bf16[256,128]{1,0:T(8,128)(2,1)S(1)} %copy-done), custom_call_target="tpu_custom_call" | custom-call | tf_op jit(solution)/shard_map/partial/pallas_call | solution.py:52
  16.3 73.4 %all_to_all.15.codes_ref = bf16[32,128,256]{2,1,0:T(8,128)(2,1)S(1)} all-to-all(bf16[32,128,256]{2,1,0:T(8,128)(2,1)S(1)} %bitcast.5), channel_id=1, replica_groups=mesh['fsdp_0'=8,'fsdp_1'=4,'fsdp_2'=2,'tensor_0'=2,'tensor_1'=4] {'fsdp_..., dimensions={0} | all-to-all | bytes 4194304 | tf_op jit(solution)/shard_map/all_to_all | solution.py:126
  89.7 1.3 %stats.1 = f32[16,8,128]{2,1,0:T(8,128)S(1)} custom-call(bf16[32,128,256]{2,1,0:T(8,128)(2,1)S(1)} %all_to_all.15.codes_ref, f32[2,128]{1,0:T(2,128)S(1)} %fusion.target_ref), custom_call_target="tpu_custom_call" | custom-call | tf_op jit(solution)/shard_map/stats/pallas_call | solution.py:52
  91.0 11.8 %all_to_all.16.parts_ref = f32[16,8,128]{2,1,0:T(8,128)S(1)} all-to-all(f32[16,8,128]{2,1,0:T(8,128)S(1)} %stats.1), channel_id=1, replica_groups=mesh['fsdp_0'=8,'fsdp_1'=4,'fsdp_2'=2,'tensor_0'=2,'tensor_1'=4] {'fsdp_..., dimensions={0} | all-to-all | bytes 131072 | tf_op jit(solution)/shard_map/all_to_all | solution.py:135
  102.9 17.8 %all_to_all.17.parts_ref = f32[32,8,128]{2,1,0:T(8,128)S(1)} all-to-all(f32[32,8,128]{2,1,0:T(8,128)S(1)} %combine.1), channel_id=1, replica_groups=mesh['fsdp_0'=8,'fsdp_1'=4,'fsdp_2'=2,'tensor_0'=2,'tensor_1'=4] {'fsdp_..., dimensions={0} | all-to-all | bytes 262144 | tf_op jit(solution)/shard_map/all_to_all | solution.py:139
  120.7 0.6 finish.1
  (4 shorter events, 0.1 us)
Async XLA Ops:
  0.6 1.7 %copy-start = (bf16[256,128]{1,0:T(8,128)(2,1)S(1)}, bf16[256,128]{1,0:T(8,128)(2,1)}, u32[]{:S(2)}) copy-start(bf16[256,128]{1,0:T(8,128)(2,1)} %hidden_ref.1) | copy-start | bytes 196612
  2.4 8.9 %copy-start.1 = (s32[256]{0:T(256)S(1)}, s32[256]{0:T(256)}, u32[]{:S(2)}) copy-start(s32[256]{0:T(256)} %param.5) | copy-start | bytes 3076
  2.5 11.6 %collective-permute-start = (bf16[4352,128]{1,0:T(8,128)(2,1)S(1)}, bf16[4352,128]{1,0:T(8,128)(2,1)S(1)}, u32[]{:S(2)}, u32[]{:S(2)}) collective-permute-start(bf16[4352,128]{1,0:T(8,128)(2,1)S(1)} %pad_maximum_fusion), channel_id=1, source_target_pairs={{0,8},{8,0},{1,9},{9,1},{2,10},{10,2},{3,11},{11,3},{4,12},{12,4},... | collective-permute-start | bytes 3342344 | tf_op jit(solution)/shard_map/ppermute | solution.py:120

commit v3 on v2

--- a/solution.py
+++ b/solution.py
@@ -9,7 +9,7 @@
 Z, Y, CORE, YL, X = "fsdp_0", "fsdp_1", "fsdp_2", "tensor_0", "tensor_1"
 FSDP = (Z, Y, CORE)
 TENSOR = (YL, X)
-OWNERS = (Z, Y)
+OWNERS = (Y, Z)
 FIRST = (Z, CORE)
 SECOND = (Y, YL, X)
 LANES = 128

time: 121 us -> 113 us (0.934)
  blocking collectives: 103 us -> 94.2 us
    all_to_all x1, blocking collectives: 73.4 us -> 63.3 us  [per_device(): lax.all_to_all(codes.reshape(peers, half // peers, tokens), OWNERS, 0, 0)]
    all_to_all x1, blocking collectives: 11.8 us -> 15 us  [per_device(): stats = lax.all_to_all(stats, FIRST, 0, 0)]
    all_to_all x1, blocking collectives: 17.8 us -> 15.9 us  [per_device(): stats = lax.all_to_all(stats, SECOND, 0, 0)]
where the time goes in v3:
time: 113 us; the launch traced here: 112 us
  blocking collectives  94.2 us (83%)
  starting transfers between devices  8.75 us (8%)
  local copies, waits for them, and re-layouts  4.32 us (4%)
  Pallas kernels  4.18 us (4%)
    all_to_all x1, blocking collectives, per_device(): lax.all_to_all(codes.reshape(peers, half // peers, tokens), OWNERS, 0, 0)  63.3 us
    all_to_all x1, blocking collectives, per_device(): stats = lax.all_to_all(stats, SECOND, 0, 0)  15.9 us
    all_to_all x1, blocking collectives, per_device(): stats = lax.all_to_all(stats, FIRST, 0, 0)  15 us
    ppermute x1, starting transfers between devices, per_device(): lax.ppermute(jnp.concatenate([others, hidden]), CORE, [(0, 1), (1, 0)])  8.75 us
    pallas_call x4, Pallas kernels, local_call(): pl.pallas_call(kernel, in_specs=specs, out_shape=results, name=name, comp...  4.18 us
    gather x1, local copies, waits for them, and re-layouts, own_target(): rows = jnp.take(head_weight, jnp.clip(local, 0, held - 1), axis=0)  2.59 us
  transfers between devices with their start and end apart: 1, of which 0 were waited for; matrix products, arithmetic and copies ran while one was open for 2% of the time, Pallas kernels for 0%

profile of v3, /device:TPU:1, one launch (start us, length us, event | category | flops | bytes accessed | tf_op | source)
XLA Modules:
  0.0 112.5 jit_solution(17615111444464300492)
XLA Ops:
  0.6 0.0 copy-start
  0.6 1.7 %constant_dynamic-slice_fusion = (bf16[4096,128]{1,0:T(8,128)(2,1)S(1)}, bf16[4096,128]{1,0:T(8,128)(2,1)S(1)}) fusion(bf16[8192,128]{1,0:T(8,128)(2,1)} %param.4, s32[]{:T(128)S(6)} %select_n.20, s32[]{:T(128)S(6)} %select_n.19), kind=kLoop, calls=%fused_computation.8 | loop fusion | bytes 4194312 | tf_op jit(solution)/shard_map/dynamic_slice | solution.py:118
  2.4 0.0 copy-start.1
  2.4 0.0 copy-done
  2.4 0.1 pad_maximum_fusion
  2.5 8.7 %collective-permute-start = (bf16[4352,128]{1,0:T(8,128)(2,1)S(1)}, bf16[4352,128]{1,0:T(8,128)(2,1)S(1)}, u32[]{:S(2)}, u32[]{:S(2)}) collective-permute-start(bf16[4352,128]{1,0:T(8,128)(2,1)S(1)} %pad_maximum_fusion), channel_id=1, source_target_pairs={{0,8},{8,0},{1,9},{9,1},{2,10},{10,2},{3,11},{11,3},{4,12},{12,4},... | collective-permute-start | bytes 3342344 | tf_op jit(solution)/shard_map/ppermute | solution.py:120
  11.2 0.0 copy-done.1
  11.3 2.6 %gather_fusion = bf16[256,128]{1,0:T(8,128)(2,1)S(1)} fusion(bf16[8192,128]{1,0:T(8,128)(2,1)} %param.4, s32[1024]{0:T(1024)S(1)} %pad_clamp_fusion), kind=kCustom, calls=%fused_computation | custom fusion | bytes 132096 | tf_op jit(solution)/shard_map/jit(_take)/gather | solution.py:107
  13.9 0.2 multiply_reduce_fusion
  14.1 0.0 collective-permute-done.swapped_ref
  14.1 2.2 %partial.1 = bf16[4096,256]{1,0:T(8,128)(2,1)S(1)} custom-call(bf16[4096,128]{1,0:T(8,128)(2,1)S(1)} %get-tuple-element.13.own_ref, bf16[4352,128]{1,0:T(8,128)(2,1)S(1)} %collective-permute-done.swapped_ref, bf16[256,128]{1,0:T(8,128)(2,1)S(1)} %copy-done), custom_call_target="tpu_custom_call" | custom-call | tf_op jit(solution)/shard_map/partial/pallas_call | solution.py:52
  16.3 63.3 %all_to_all.15.codes_ref = bf16[32,128,256]{2,1,0:T(8,128)(2,1)S(1)} all-to-all(bf16[32,128,256]{2,1,0:T(8,128)(2,1)S(1)} %bitcast.5), channel_id=1, replica_groups=mesh['fsdp_0'=8,'fsdp_1'=4,'fsdp_2'=2,'tensor_0'=2,'tensor_1'=4] {'fsdp_..., dimensions={0} | all-to-all | bytes 4194304 | tf_op jit(solution)/shard_map/all_to_all | solution.py:126
  79.6 1.3 %stats.1 = f32[16,8,128]{2,1,0:T(8,128)S(1)} custom-call(bf16[32,128,256]{2,1,0:T(8,128)(2,1)S(1)} %all_to_all.15.codes_ref, f32[2,128]{1,0:T(2,128)S(1)} %fusion.target_ref), custom_call_target="tpu_custom_call" | custom-call | tf_op jit(solution)/shard_map/stats/pallas_call | solution.py:52
  80.9 15.0 %all_to_all.16.parts_ref = f32[16,8,128]{2,1,0:T(8,128)S(1)} all-to-all(f32[16,8,128]{2,1,0:T(8,128)S(1)} %stats.1), channel_id=1, replica_groups=mesh['fsdp_0'=8,'fsdp_1'=4,'fsdp_2'=2,'tensor_0'=2,'tensor_1'=4] {'fsdp_..., dimensions={0} | all-to-all | bytes 131072 | tf_op jit(solution)/shard_map/all_to_all | solution.py:135
  96.0 15.9 %all_to_all.17.parts_ref = f32[32,8,128]{2,1,0:T(8,128)S(1)} all-to-all(f32[32,8,128]{2,1,0:T(8,128)S(1)} %combine.1), channel_id=1, replica_groups=mesh['fsdp_0'=8,'fsdp_1'=4,'fsdp_2'=2,'tensor_0'=2,'tensor_1'=4] {'fsdp_..., dimensions={0} | all-to-all | bytes 262144 | tf_op jit(solution)/shard_map/all_to_all | solution.py:139
  111.8 0.6 finish.1
  (4 shorter events, 0.1 us)
Async XLA Ops:
  0.6 1.7 %copy-start = (bf16[256,128]{1,0:T(8,128)(2,1)S(1)}, bf16[256,128]{1,0:T(8,128)(2,1)}, u32[]{:S(2)}) copy-start(bf16[256,128]{1,0:T(8,128)(2,1)} %hidden_ref.1) | copy-start | bytes 196612
  2.4 8.9 %copy-start.1 = (s32[256]{0:T(256)S(1)}, s32[256]{0:T(256)}, u32[]{:S(2)}) copy-start(s32[256]{0:T(256)} %param.5) | copy-start | bytes 3076
  2.5 11.6 %collective-permute-start = (bf16[4352,128]{1,0:T(8,128)(2,1)S(1)}, bf16[4352,128]{1,0:T(8,128)(2,1)S(1)}, u32[]{:S(2)}, u32[]{:S(2)}) collective-permute-start(bf16[4352,128]{1,0:T(8,128)(2,1)S(1)} %pad_maximum_fusion), channel_id=1, source_target_pairs={{0,8},{8,0},{1,9},{9,1},{2,10},{10,2},{3,11},{11,3},{4,12},{12,4},... | collective-permute-start | bytes 3342344 | tf_op jit(solution)/shard_map/ppermute | solution.py:120

commit v4 on v3

--- a/solution.py
+++ b/solution.py
@@ -1,3 +1,5 @@
+import functools
+
 import jax
 import jax.numpy as jnp
 from jax import lax
@@ -9,24 +11,35 @@
 Z, Y, CORE, YL, X = "fsdp_0", "fsdp_1", "fsdp_2", "tensor_0", "tensor_1"
 FSDP = (Z, Y, CORE)
 TENSOR = (YL, X)
-OWNERS = (Y, Z)
+ALL = FSDP + TENSOR
 FIRST = (Z, CORE)
 SECOND = (Y, YL, X)
 LANES = 128
 
 
+REACH = 25
+
+
 def encode(value):
-    square = value * jnp.abs(value)
-    return (square * jnp.abs(square)).astype(jnp.bfloat16)
+    square = value * value
+    return (square * square * value).astype(jnp.bfloat16)
 
 
 def decode(code):
     code = code.astype(jnp.float32)
-    root = lax.rsqrt(lax.rsqrt(jnp.abs(code)))
-    return jnp.where(code < 0, -root, root)
-
-
-def partial_kernel(own_ref, swapped_ref, hidden_ref, out_ref):
+    size = jnp.abs(code)
+    root = jnp.exp2(jnp.log2(jnp.maximum(size, 2.0**-126)) * 0.2)
+    return jnp.where(code < 0, -root, jnp.where(code > 0, root, 0.0))
+
+
+def decoded_sum(codes_ref, at):
+    total = decode(codes_ref[0, at, :])
+    for peer in range(1, codes_ref.shape[0]):
+        total = total + decode(codes_ref[peer, at, :])
+    return total
+
+
+def partial_kernel(scale, own_ref, swapped_ref, hidden_ref, out_ref):
     half, depth = own_ref.shape
     tokens = hidden_ref.shape[0]
     hidden = jnp.concatenate([hidden_ref[...], swapped_ref[half : half + tokens, :]], axis=1)
@@ -38,7 +51,7 @@
         logits = lax.dot_general(
             rows, hidden, (((1,), (1,)), ((), ())), preferred_element_type=jnp.float32
         )
-        out_ref[at, :] = encode(logits)
+        out_ref[at, :] = encode(logits * scale)
         return carry
 
     lax.fori_loop(0, half // step, add_rows, 0)
@@ -65,15 +78,24 @@
     return jnp.concatenate([row[:, :LANES], row[:, LANES:]], axis=0)
 
 
-def stats_kernel(codes_ref, target_ref, out_ref, logits_ref):
-    peers, rows, tokens = codes_ref.shape
+def sum_kernel(scale, codes_ref, out_ref):
+    step = 32
+
+    def add_rows(k, carry):
+        at = pl.ds(pl.multiple_of(k * step, step), step)
+        out_ref[at, :] = encode(decoded_sum(codes_ref, at) * scale)
+        return carry
+
+    lax.fori_loop(0, out_ref.shape[0] // step, add_rows, 0)
+
+
+def stats_kernel(scale, codes_ref, target_ref, out_ref, logits_ref):
+    rows, tokens = logits_ref.shape
     step = 32
 
     def add_rows(k, peak):
         at = pl.ds(pl.multiple_of(k * step, step), step)
-        total = decode(codes_ref[0, at, :])
-        for peer in range(1, peers):
-            total = total + decode(codes_ref[peer, at, :])
+        total = decoded_sum(codes_ref, at) * scale
         logits_ref[at, :] = total
         return jnp.maximum(peak, jnp.max(total, axis=0, keepdims=True))
 
@@ -109,28 +131,59 @@
     return jnp.where((local >= 0) & (local < held), share, 0.0)
 
 
+def round_groups(deep, high, tensor):
+    def at(z, y, core, rest):
+        return ((z * high + y) * 2 + core) * tensor + rest
+
+    one, two = [], []
+    for rest in range(tensor):
+        for parity in range(2):
+            for y in range(high):
+                one.append([at(z, y, 0, rest) for z in range(parity, deep, 2)])
+        for z in range(deep):
+            one.append([at(z, y, 1, rest) for y in range(high)])
+        for pair in range(0, deep, 2):
+            two.append([at(z, y, 0, rest) for y in range(high) for z in (pair, pair + 1)])
+        for y in range(high):
+            two.append([at(z, y, 1, rest) for z in range(deep)])
+    return one, two
+
+
 def per_device(hidden, head_weight, targets):
     held = head_weight.shape[0]
     tokens = hidden.shape[0]
     half = held // 2
-    peers = lax.axis_size(OWNERS)
+    deep, high = lax.axis_size(Z), lax.axis_size(Y)
+    one, two = round_groups(deep, high, lax.axis_size(TENSOR))
     core = lax.axis_index(CORE)
     others = lax.dynamic_slice_in_dim(head_weight, (1 - core) * half, half, axis=0)
     own = lax.dynamic_slice_in_dim(head_weight, core * half, half, axis=0)
     swapped = lax.ppermute(jnp.concatenate([others, hidden]), CORE, [(0, 1), (1, 0)])
     (codes,) = local_call(
-        partial_kernel, "partial", [((half, tokens), jnp.bfloat16)], own, swapped, hidden
+        functools.partial(partial_kernel, 2.0 ** (REACH - 15)),
+        "partial",
+        [((half, tokens), jnp.bfloat16)],
+        own,
+        swapped,
+        hidden,
     )
     target = own_target(hidden, head_weight, targets).reshape(2, LANES)
     codes, target = lax.optimization_barrier((codes, target))
-    codes = lax.all_to_all(codes.reshape(peers, half // peers, tokens), OWNERS, 0, 0)
+    rows = half // high
+    codes = codes.reshape(high, rows, tokens)
+    codes = lax.all_to_all(codes, ALL, 0, 0, axis_index_groups=one)
+    (codes,) = local_call(
+        functools.partial(sum_kernel, 2.0**-2), "sum", [((rows, tokens), jnp.bfloat16)], codes
+    )
+    codes = codes.reshape(deep, rows // deep, tokens)
+    codes = lax.all_to_all(codes, ALL, 0, 0, axis_index_groups=two)
     (stats,) = local_call(
-        stats_kernel,
+        functools.partial(stats_kernel, 2.0 ** (17 - REACH)),
         "stats",
         [((lax.axis_size(FIRST), 8, LANES), jnp.float32)],
         codes,
         target,
-        scratch_shapes=[pltpu.VMEM((half // peers, tokens), jnp.float32)],
+        scratch_shapes=[pltpu.VMEM((rows // deep, tokens), jnp.float32)],
     )
     stats = lax.all_to_all(stats, FIRST, 0, 0)
     (stats,) = local_call(

time: 113 us -> 100 us (0.88)
  blocking collectives: 94.2 us -> 80.2 us
  Pallas kernels: 4.18 us -> 5.63 us
    all_to_all x1 -> x2, blocking collectives: 63.3 us -> 53.2 us  [the longest x1 29.5 us: per_device(): codes = lax.all_to_all(codes, ALL, 0, 0, axis_index_groups=one)]
    all_to_all x1, blocking collectives: 15 us -> 11.2 us  [per_device(): stats = lax.all_to_all(stats, FIRST, 0, 0)]
    pallas_call x4 -> x5, Pallas kernels: 4.18 us -> 5.63 us  [local_call(): pl.pallas_call(kernel, in_specs=specs, out_shape=results, name=name, comp...]
  transfers between devices with their start and end apart: 1 -> 1, of which waited for: 0 -> 0; matrix products, arithmetic and copies ran while one was open for 2% -> 3% of each run, Pallas kernels for 0% -> 0%
where the time goes in v4:
time: 100 us
  blocking collectives  80.2 us (80%)
  starting transfers between devices  8.75 us (9%)
  Pallas kernels  5.63 us (6%)
  local copies, waits for them, and re-layouts  4.32 us (4%)
    all_to_all x1, blocking collectives, per_device(): codes = lax.all_to_all(codes, ALL, 0, 0, axis_index_groups=one)  29.5 us
    all_to_all x1, blocking collectives, per_device(): codes = lax.all_to_all(codes, ALL, 0, 0, axis_index_groups=two)  23.7 us
    all_to_all x1, blocking collectives, per_device(): stats = lax.all_to_all(stats, SECOND, 0, 0)  15.9 us
    all_to_all x1, blocking collectives, per_device(): stats = lax.all_to_all(stats, FIRST, 0, 0)  11.2 us
    ppermute x1, starting transfers between devices, per_device(): lax.ppermute(jnp.concatenate([others, hidden]), CORE, [(0, 1), (1, 0)])  8.75 us
    pallas_call x5, Pallas kernels, local_call(): pl.pallas_call(kernel, in_specs=specs, out_shape=results, name=name, comp...  5.63 us
    gather x1, local copies, waits for them, and re-layouts, own_target(): rows = jnp.take(head_weight, jnp.clip(local, 0, held - 1), axis=0)  2.59 us
  transfers between devices with their start and end apart: 1, of which 0 were waited for; matrix products, arithmetic and copies ran while one was open for 3% of the time, Pallas kernels for 0%

profile of v4, /device:TPU:1, one launch (start us, length us, event | category | flops | bytes accessed | tf_op | source)
XLA Modules:
  0.0 100.0 jit_solution(4635778738042674230)
XLA Ops:
  0.6 0.0 copy-start
  0.6 1.7 %constant_dynamic-slice_fusion = (bf16[4096,128]{1,0:T(8,128)(2,1)S(1)}, bf16[4096,128]{1,0:T(8,128)(2,1)S(1)}) fusion(bf16[8192,128]{1,0:T(8,128)(2,1)} %param.4, s32[]{:T(128)S(6)} %select_n.20, s32[]{:T(128)S(6)} %select_n.19), kind=kLoop, calls=%fused_computation.8 | loop fusion | bytes 4194312 | tf_op jit(solution)/shard_map/dynamic_slice | solution.py:159
  2.4 0.0 copy-start.1
  2.4 0.0 copy-done
  2.4 0.1 pad_maximum_fusion
  2.5 8.7 %collective-permute-start = (bf16[4352,128]{1,0:T(8,128)(2,1)S(1)}, bf16[4352,128]{1,0:T(8,128)(2,1)S(1)}, u32[]{:S(2)}, u32[]{:S(2)}) collective-permute-start(bf16[4352,128]{1,0:T(8,128)(2,1)S(1)} %pad_maximum_fusion), channel_id=1, source_target_pairs={{0,8},{8,0},{1,9},{9,1},{2,10},{10,2},{3,11},{11,3},{4,12},{12,4},... | collective-permute-start | bytes 3342344 | tf_op jit(solution)/shard_map/ppermute | solution.py:161
  11.2 0.0 copy-done.1
  11.3 2.6 %gather_fusion = bf16[256,128]{1,0:T(8,128)(2,1)S(1)} fusion(bf16[8192,128]{1,0:T(8,128)(2,1)} %param.4, s32[1024]{0:T(1024)S(1)} %pad_clamp_fusion), kind=kCustom, calls=%fused_computation | custom fusion | bytes 132096 | tf_op jit(solution)/shard_map/jit(_take)/gather | solution.py:129
  13.9 0.2 multiply_reduce_fusion
  14.1 0.0 collective-permute-done.swapped_ref
  14.1 2.2 %partial.1 = bf16[4096,256]{1,0:T(8,128)(2,1)S(1)} custom-call(bf16[4096,128]{1,0:T(8,128)(2,1)S(1)} %get-tuple-element.13.own_ref, bf16[4352,128]{1,0:T(8,128)(2,1)S(1)} %collective-permute-done.swapped_ref, bf16[256,128]{1,0:T(8,128)(2,1)S(1)} %copy-done), custom_call_target="tpu_custom_call" | custom-call | tf_op jit(solution)/shard_map/partial/pallas_call | solution.py:65
  16.3 29.5 %all_to_all.20.codes_ref = bf16[4,1024,256]{2,1,0:T(8,128)(2,1)S(1)} all-to-all(bf16[4,1024,256]{2,1,0:T(8,128)(2,1)S(1)} %bitcast.6), channel_id=1, replica_groups={{0,128,256,384},{16,144,272,400},{32,160,288,416},{48,176,304,432},{64,..., dimensions={0} | all-to-all | bytes 4194304 | tf_op jit(solution)/shard_map/all_to_all | solution.py:174
  45.8 2.2 %sum.1 = bf16[1024,256]{1,0:T(8,128)(2,1)S(1)} custom-call(bf16[4,1024,256]{2,1,0:T(8,128)(2,1)S(1)} %all_to_all.20.codes_ref), custom_call_target="tpu_custom_call" | custom-call | tf_op jit(solution)/shard_map/sum/pallas_call | solution.py:65
  48.0 23.7 %all_to_all.21.codes_ref = bf16[8,128,256]{2,1,0:T(8,128)(2,1)S(1)} all-to-all(bf16[8,128,256]{2,1,0:T(8,128)(2,1)S(1)} %bitcast.7), channel_id=1, replica_groups={{0,64,16,80,32,96,48,112},{128,192,144,208,160,224,176,240},{256,320,27..., dimensions={0} | all-to-all | bytes 1048576 | tf_op jit(solution)/shard_map/all_to_all | solution.py:179
  71.7 0.5 stats.1
  72.2 11.2 %all_to_all.22.parts_ref = f32[16,8,128]{2,1,0:T(8,128)S(1)} all-to-all(f32[16,8,128]{2,1,0:T(8,128)S(1)} %stats.1), channel_id=1, replica_groups=mesh['fsdp_0'=8,'fsdp_1'=4,'fsdp_2'=2,'tensor_0'=2,'tensor_1'=4] {'fsdp_..., dimensions={0} | all-to-all | bytes 131072 | tf_op jit(solution)/shard_map/all_to_all | solution.py:188
  83.4 15.9 %all_to_all.23.parts_ref = f32[32,8,128]{2,1,0:T(8,128)S(1)} all-to-all(f32[32,8,128]{2,1,0:T(8,128)S(1)} %combine.1), channel_id=1, replica_groups=mesh['fsdp_0'=8,'fsdp_1'=4,'fsdp_2'=2,'tensor_0'=2,'tensor_1'=4] {'fsdp_..., dimensions={0} | all-to-all | bytes 262144 | tf_op jit(solution)/shard_map/all_to_all | solution.py:192
  99.3 0.6 finish.1
  (4 shorter events, 0.1 us)
Async XLA Ops:
  0.6 1.7 %copy-start = (bf16[256,128]{1,0:T(8,128)(2,1)S(1)}, bf16[256,128]{1,0:T(8,128)(2,1)}, u32[]{:S(2)}) copy-start(bf16[256,128]{1,0:T(8,128)(2,1)} %hidden_ref.1) | copy-start | bytes 196612
  2.4 8.9 %copy-start.1 = (s32[256]{0:T(256)S(1)}, s32[256]{0:T(256)}, u32[]{:S(2)}) copy-start(s32[256]{0:T(256)} %param.5) | copy-start | bytes 3076
  2.5 11.6 %collective-permute-start = (bf16[4352,128]{1,0:T(8,128)(2,1)S(1)}, bf16[4352,128]{1,0:T(8,128)(2,1)S(1)}, u32[]{:S(2)}, u32[]{:S(2)}) collective-permute-start(bf16[4352,128]{1,0:T(8,128)(2,1)S(1)} %pad_maximum_fusion), channel_id=1, source_target_pairs={{0,8},{8,0},{1,9},{9,1},{2,10},{10,2},{3,11},{11,3},{4,12},{12,4},... | collective-permute-start | bytes 3342344 | tf_op jit(solution)/shard_map/ppermute | solution.py:161

commit v5 on v4

--- a/solution.py
+++ b/solution.py
@@ -12,23 +12,23 @@
 FSDP = (Z, Y, CORE)
 TENSOR = (YL, X)
 ALL = FSDP + TENSOR
-FIRST = (Z, CORE)
-SECOND = (Y, YL, X)
+FIRST = (CORE, Z)
+SECOND = (X, YL, Y)
 LANES = 128
 
 
-REACH = 25
+REACH = 20
 
 
 def encode(value):
-    square = value * value
-    return (square * square * value).astype(jnp.bfloat16)
+    cube = value * value * value
+    return (cube * jnp.abs(cube)).astype(jnp.bfloat16)
 
 
 def decode(code):
     code = code.astype(jnp.float32)
     size = jnp.abs(code)
-    root = jnp.exp2(jnp.log2(jnp.maximum(size, 2.0**-126)) * 0.2)
+    root = jnp.exp2(jnp.log2(jnp.maximum(size, 2.0**-126)) * (1 / 6))
     return jnp.where(code < 0, -root, jnp.where(code > 0, root, 0.0))
 
 
@@ -54,7 +54,7 @@
         out_ref[at, :] = encode(logits * scale)
         return carry
 
-    lax.fori_loop(0, half // step, add_rows, 0)
+    lax.fori_loop(0, half // step, add_rows, 0, unroll=True)
 
 
 def local_call(kernel, name, out, *operands, place=pltpu.VMEM, **more):
@@ -86,24 +86,27 @@
         out_ref[at, :] = encode(decoded_sum(codes_ref, at) * scale)
         return carry
 
-    lax.fori_loop(0, out_ref.shape[0] // step, add_rows, 0)
-
-
-def stats_kernel(scale, codes_ref, target_ref, out_ref, logits_ref):
+    lax.fori_loop(0, out_ref.shape[0] // step, add_rows, 0, unroll=4)
+
+
+def stats_kernel(scale, codes_ref, target_row_ref, out_ref, logits_ref):
     rows, tokens = logits_ref.shape
     step = 32
 
-    def add_rows(k, peak):
+    def add_rows(k, state):
+        peak, target = state
         at = pl.ds(pl.multiple_of(k * step, step), step)
         total = decoded_sum(codes_ref, at) * scale
         logits_ref[at, :] = total
-        return jnp.maximum(peak, jnp.max(total, axis=0, keepdims=True))
-
-    peak = lax.fori_loop(
-        0, rows // step, add_rows, jnp.full((1, tokens), -jnp.inf, jnp.float32)
-    )
+        peak = jnp.maximum(peak, jnp.max(total, axis=0, keepdims=True))
+        row = lax.broadcasted_iota(jnp.int32, total.shape, 0) + k * step
+        matched = jnp.where(row == target_row_ref[...], total, 0.0)
+        return peak, target + jnp.sum(matched, axis=0, keepdims=True)
+
+    start = jnp.full((1, tokens), -jnp.inf, jnp.float32), jnp.zeros((1, tokens), jnp.float32)
+    peak, target = lax.fori_loop(0, rows // step, add_rows, start, unroll=True)
     expsum = jnp.sum(jnp.exp(logits_ref[...] - peak), axis=0, keepdims=True)
-    put_stats(out_ref, two_rows(peak), two_rows(expsum), target_ref[...])
+    put_stats(out_ref, two_rows(peak), two_rows(expsum), two_rows(target))
 
 
 def combine(parts):
@@ -121,14 +124,6 @@
     peak, expsum, target = combine(parts_ref[...])
     logprob_ref[...] = target - peak - jnp.log(expsum)
     gap_ref[...] = target - peak
-
-
-def own_target(hidden, head_weight, targets):
-    held = head_weight.shape[0]
-    local = targets - lax.axis_index(TENSOR) * held
-    rows = jnp.take(head_weight, jnp.clip(local, 0, held - 1), axis=0)
-    share = jnp.sum(rows.astype(jnp.float32) * hidden.astype(jnp.float32), axis=1)
-    return jnp.where((local >= 0) & (local < held), share, 0.0)
 
 
 def round_groups(deep, high, tensor):
@@ -143,7 +138,7 @@
         for z in range(deep):
             one.append([at(z, y, 1, rest) for y in range(high)])
         for pair in range(0, deep, 2):
-            two.append([at(z, y, 0, rest) for y in range(high) for z in (pair, pair + 1)])
+            two.append([at(z, y, 0, rest) for z in (pair, pair + 1) for y in range(high)])
         for y in range(high):
             two.append([at(z, y, 1, rest) for z in range(deep)])
     return one, two
@@ -167,9 +162,13 @@
         swapped,
         hidden,
     )
-    target = own_target(hidden, head_weight, targets).reshape(2, LANES)
-    codes, target = lax.optimization_barrier((codes, target))
     rows = half // high
+    z, y = lax.axis_index(Z), lax.axis_index(Y)
+    chunk = jnp.where(core == 0, z // 2, y)
+    piece = jnp.where(core == 0, z % 2 * high + y, z)
+    first_row = lax.axis_index(TENSOR) * held + core * half + chunk * rows + piece * (rows // deep)
+    target_row = (targets - first_row).reshape(1, tokens)
+    codes, target_row = lax.optimization_barrier((codes, target_row))
     codes = codes.reshape(high, rows, tokens)
     codes = lax.all_to_all(codes, ALL, 0, 0, axis_index_groups=one)
     (codes,) = local_call(
@@ -182,7 +181,7 @@
         "stats",
         [((lax.axis_size(FIRST), 8, LANES), jnp.float32)],
         codes,
-        target,
+        target_row,
         scratch_shapes=[pltpu.VMEM((rows // deep, tokens), jnp.float32)],
     )
     stats = lax.all_to_all(stats, FIRST, 0, 0)

time: 100 us -> 97.5 us (0.975)
  local copies, waits for them, and re-layouts: 4.32 us -> 1.72 us
  waiting for transfers between devices: 0.01 us -> 2.3 us
  Pallas kernels: 5.63 us -> 3.97 us
  blocking collectives: 80.2 us -> 79.1 us
    gather x1 -> x0, local copies, waits for them, and re-layouts: 2.59 us -> none  [own_target(): rows = jnp.take(head_weight, jnp.clip(local, 0, held - 1), axis=0)]
    ppermute x1, waiting for transfers between devices: 0.01 us -> 2.3 us  [per_device(): lax.ppermute(jnp.concatenate([others, hidden]), CORE, [(0, 1), (1, 0)])]
    pallas_call x5, Pallas kernels: 5.63 us -> 3.97 us  [local_call(): pl.pallas_call(kernel, in_specs=specs, out_shape=results, name=name, comp...]
    all_to_all x1, blocking collectives: 15.9 us -> 14.8 us  [per_device(): stats = lax.all_to_all(stats, SECOND, 0, 0)]
  transfers between devices with their start and end apart: 1 -> 1, of which waited for: 0 -> 1; matrix products, arithmetic and copies ran while one was open for 3% -> 0% of each run, Pallas kernels for 0% -> 0%
where the time goes in v5:
time: 97.5 us; the launch traced here: 96.7 us
  blocking collectives  79.1 us (81%)
  starting transfers between devices  8.75 us (9%)
  Pallas kernels  3.97 us (4%)
  waiting for transfers between devices  2.3 us (2%)
  local copies, waits for them, and re-layouts  1.72 us (2%)
    all_to_all x1, blocking collectives, per_device(): codes = lax.all_to_all(codes, ALL, 0, 0, axis_index_groups=one)  29.5 us
    all_to_all x1, blocking collectives, per_device(): codes = lax.all_to_all(codes, ALL, 0, 0, axis_index_groups=two)  23.3 us
    all_to_all x1, blocking collectives, per_device(): stats = lax.all_to_all(stats, SECOND, 0, 0)  14.8 us
    all_to_all x1, blocking collectives, per_device(): stats = lax.all_to_all(stats, FIRST, 0, 0)  11.5 us
    ppermute x1, starting transfers between devices, per_device(): lax.ppermute(jnp.concatenate([others, hidden]), CORE, [(0, 1), (1, 0)])  8.75 us
    pallas_call x5, Pallas kernels, local_call(): pl.pallas_call(kernel, in_specs=specs, out_shape=results, name=name, comp...  3.97 us
    ppermute x1, waiting for transfers between devices, per_device(): lax.ppermute(jnp.concatenate([others, hidden]), CORE, [(0, 1), (1, 0)])  2.3 us
  transfers between devices with their start and end apart: 1, of which 1 were waited for; matrix products, arithmetic and copies ran while one was open for 0% of the time, Pallas kernels for 0%

profile of v5, /device:TPU:1, one launch (start us, length us, event | category | flops | bytes accessed | tf_op | source)
XLA Modules:
  0.0 96.7 jit_solution(6133329808677716596)
XLA Ops:
  0.6 0.0 copy-start
  0.6 1.7 %constant_dynamic-slice_fusion = (bf16[4096,128]{1,0:T(8,128)(2,1)S(1)}, bf16[4096,128]{1,0:T(8,128)(2,1)S(1)}) fusion(bf16[8192,128]{1,0:T(8,128)(2,1)} %param.4, s32[]{:T(128)S(6)} %select_n.24, s32[]{:T(128)S(6)} %select_n.23), kind=kLoop, calls=%fused_computation.2 | loop fusion | bytes 4194312 | tf_op jit(solution)/shard_map/dynamic_slice | solution.py:154
  2.4 0.0 copy-start.1
  2.4 0.0 copy-done
  2.4 0.1 pad_maximum_fusion
  2.5 8.7 %collective-permute-start = (bf16[4352,128]{1,0:T(8,128)(2,1)S(1)}, bf16[4352,128]{1,0:T(8,128)(2,1)S(1)}, u32[]{:S(2)}, u32[]{:S(2)}) collective-permute-start(bf16[4352,128]{1,0:T(8,128)(2,1)S(1)} %pad_maximum_fusion), channel_id=1, source_target_pairs={{0,8},{8,0},{1,9},{9,1},{2,10},{10,2},{3,11},{11,3},{4,12},{12,4},... | collective-permute-start | bytes 3342344 | tf_op jit(solution)/shard_map/ppermute | solution.py:156
  11.3 0.0 copy-done.1
  11.3 2.3 %collective-permute-done.swapped_ref = bf16[4352,128]{1,0:T(8,128)(2,1)S(1)} collective-permute-done((bf16[4352,128]{1,0:T(8,128)(2,1)S(1)}, bf16[4352,128]{1,0:T(8,128)(2,1)S(1)}, u32[]{:S(2)}, u32[]{:S(2)}) %collective-permute-start) | collective-permute-done | bytes 1114144 | tf_op jit(solution)/shard_map/ppermute | solution.py:156
  13.6 1.0 partial.1
  14.5 29.5 %all_to_all.20.codes_ref = bf16[4,1024,256]{2,1,0:T(8,128)(2,1)S(1)} all-to-all(bf16[4,1024,256]{2,1,0:T(8,128)(2,1)S(1)} %bitcast.5), channel_id=1, replica_groups={{0,128,256,384},{16,144,272,400},{32,160,288,416},{48,176,304,432},{64,..., dimensions={0} | all-to-all | bytes 4194304 | tf_op jit(solution)/shard_map/all_to_all | solution.py:173
  44.0 1.9 %sum.1 = bf16[1024,256]{1,0:T(8,128)(2,1)S(1)} custom-call(bf16[4,1024,256]{2,1,0:T(8,128)(2,1)S(1)} %all_to_all.20.codes_ref), custom_call_target="tpu_custom_call" | custom-call | tf_op jit(solution)/shard_map/sum/pallas_call | solution.py:65
  45.9 23.3 %all_to_all.21.codes_ref = bf16[8,128,256]{2,1,0:T(8,128)(2,1)S(1)} all-to-all(bf16[8,128,256]{2,1,0:T(8,128)(2,1)S(1)} %bitcast.6), channel_id=1, replica_groups={{0,16,32,48,64,80,96,112},{128,144,160,176,192,208,224,240},{256,272,28..., dimensions={0} | all-to-all | bytes 1048576 | tf_op jit(solution)/shard_map/all_to_all | solution.py:178
  69.2 0.5 stats.1
  69.7 11.5 %all_to_all.22.parts_ref = f32[16,8,128]{2,1,0:T(8,128)S(1)} all-to-all(f32[16,8,128]{2,1,0:T(8,128)S(1)} %stats.1), channel_id=1, replica_groups=mesh['fsdp_0'=8,'fsdp_1'=4,'fsdp_2'=2,'tensor_0'=2,'tensor_1'=4] {'fsdp_..., dimensions={0} | all-to-all | bytes 131072 | tf_op jit(solution)/shard_map/all_to_all | solution.py:187
  81.2 14.8 %all_to_all.23.parts_ref = f32[32,8,128]{2,1,0:T(8,128)S(1)} all-to-all(f32[32,8,128]{2,1,0:T(8,128)S(1)} %combine.1), channel_id=1, replica_groups=mesh['fsdp_0'=8,'fsdp_1'=4,'fsdp_2'=2,'tensor_0'=2,'tensor_1'=4] {'tenso..., dimensions={0} | all-to-all | bytes 262144 | tf_op jit(solution)/shard_map/all_to_all | solution.py:191
  96.0 0.6 finish.1
  (2 shorter events, 0.0 us)
Async XLA Ops:
  0.6 1.7 %copy-start = (bf16[256,128]{1,0:T(8,128)(2,1)S(1)}, bf16[256,128]{1,0:T(8,128)(2,1)}, u32[]{:S(2)}) copy-start(bf16[256,128]{1,0:T(8,128)(2,1)} %hidden_ref.1) | copy-start | bytes 196612
  2.4 8.9 %copy-start.1 = (s32[256]{0:T(256)S(1)}, s32[256]{0:T(256)}, u32[]{:S(2)}) copy-start(s32[256]{0:T(256)} %param.5) | copy-start | bytes 3076
  2.5 11.1 %collective-permute-start = (bf16[4352,128]{1,0:T(8,128)(2,1)S(1)}, bf16[4352,128]{1,0:T(8,128)(2,1)S(1)}, u32[]{:S(2)}, u32[]{:S(2)}) collective-permute-start(bf16[4352,128]{1,0:T(8,128)(2,1)S(1)} %pad_maximum_fusion), channel_id=1, source_target_pairs={{0,8},{8,0},{1,9},{9,1},{2,10},{10,2},{3,11},{11,3},{4,12},{12,4},... | collective-permute-start | bytes 3342344 | tf_op jit(solution)/shard_map/ppermute | solution.py:156

commit v6 on v5

--- a/solution.py
+++ b/solution.py
@@ -27,9 +27,8 @@
 
 def decode(code):
     code = code.astype(jnp.float32)
-    size = jnp.abs(code)
-    root = jnp.exp2(jnp.log2(jnp.maximum(size, 2.0**-126)) * (1 / 6))
-    return jnp.where(code < 0, -root, jnp.where(code > 0, root, 0.0))
+    size = jnp.maximum(jnp.abs(code), 2.0**-126)
+    return code * jnp.exp2(jnp.log2(size) * (-5 / 6))
 
 
 def decoded_sum(codes_ref, at):
@@ -37,6 +36,30 @@
     for peer in range(1, codes_ref.shape[0]):
         total = total + decode(codes_ref[peer, at, :])
     return total
+
+
+def pick_kernel(weight_ref, hidden_ref, out_ref, sems):
+    half = weight_ref.shape[0] // 2
+    start = (1 - lax.axis_index(CORE)) * half
+    rows = pltpu.make_async_copy(
+        weight_ref.at[pl.ds(pl.multiple_of(start, half), half)], out_ref.at[:half], sems.at[0]
+    )
+    features = pltpu.make_async_copy(hidden_ref, out_ref.at[half:], sems.at[1])
+    rows.start()
+    features.start()
+    rows.wait()
+    features.wait()
+
+
+def pick(head_weight, hidden):
+    rows = head_weight.shape[0] // 2 + hidden.shape[0]
+    return pl.pallas_call(
+        pick_kernel,
+        in_specs=[pl.BlockSpec(memory_space=pl.ANY)] * 2,
+        out_shape=pltpu.VMEM((rows, hidden.shape[1]), hidden.dtype),
+        scratch_shapes=[pltpu.SemaphoreType.DMA((2,))],
+        name="pick",
+    )(head_weight, hidden)
 
 
 def partial_kernel(scale, own_ref, swapped_ref, hidden_ref, out_ref):
@@ -151,9 +174,8 @@
     deep, high = lax.axis_size(Z), lax.axis_size(Y)
     one, two = round_groups(deep, high, lax.axis_size(TENSOR))
     core = lax.axis_index(CORE)
-    others = lax.dynamic_slice_in_dim(head_weight, (1 - core) * half, half, axis=0)
     own = lax.dynamic_slice_in_dim(head_weight, core * half, half, axis=0)
-    swapped = lax.ppermute(jnp.concatenate([others, hidden]), CORE, [(0, 1), (1, 0)])
+    swapped = lax.ppermute(pick(head_weight, hidden), CORE, [(0, 1), (1, 0)])
     (codes,) = local_call(
         functools.partial(partial_kernel, 2.0 ** (REACH - 15)),
         "partial",

time: 97.5 us -> 96.5 us (0.990)
  waiting for transfers between devices: 2.3 us -> 1 us
    ppermute x1, waiting for transfers between devices: 2.3 us -> 1 us  [per_device(): swapped = lax.ppermute(pick(head_weight, hidden), CORE, [(0, 1), (1, 0)])]
    pallas_call x0 -> x1, Pallas kernels: none -> 1.27 us  [pick(): pl.pallas_call(pick_kernel, in_specs=[pl.BlockSpec(memory_space=pl.ANY)]...]
  transfers between devices with their start and end apart: 1 -> 1, of which waited for: 1 -> 1; matrix products, arithmetic and copies ran while one was open for 0% -> 1% of each run, Pallas kernels for 0% -> 0%
where the time goes in v6:
time: 96.5 us; the launch traced here: 95.6 us
  blocking collectives  79.2 us (82%)
  starting transfers between devices  8.75 us (9%)
  Pallas kernels  4.68 us (5%)
  local copies, waits for them, and re-layouts  1.31 us (1%)
  waiting for transfers between devices  1 us (1%)
    all_to_all x1, blocking collectives, per_device(): codes = lax.all_to_all(codes, ALL, 0, 0, axis_index_groups=one)  29.5 us
    all_to_all x1, blocking collectives, per_device(): codes = lax.all_to_all(codes, ALL, 0, 0, axis_index_groups=two)  23.3 us
    all_to_all x1, blocking collectives, per_device(): stats = lax.all_to_all(stats, SECOND, 0, 0)  14.9 us
    all_to_all x1, blocking collectives, per_device(): stats = lax.all_to_all(stats, FIRST, 0, 0)  11.5 us
    ppermute x1, starting transfers between devices, per_device(): swapped = lax.ppermute(pick(head_weight, hidden), CORE, [(0, 1), (1, 0)])  8.75 us
    pallas_call x5, Pallas kernels, local_call(): pl.pallas_call(kernel, in_specs=specs, out_shape=results, name=name, comp...  3.41 us
  transfers between devices with their start and end apart: 1, of which 1 were waited for; matrix products, arithmetic and copies ran while one was open for 1% of the time, Pallas kernels for 0%

profile of v6, /device:TPU:1, one launch (start us, length us, event | category | flops | bytes accessed | tf_op | source)
XLA Modules:
  0.0 95.6 jit_solution(2906698384731273587)
XLA Ops:
  0.6 0.0 copy-start
  0.6 0.0 copy-start.1
  0.6 1.3 %pick.1 = bf16[4352,128]{1,0:T(8,128)(2,1)S(1)} custom-call(bf16[8192,128]{1,0:T(8,128)(2,1)} %weight_ref.1, bf16[256,128]{1,0:T(8,128)(2,1)} %hidden_ref.3), custom_call_target="tpu_custom_call" | custom-call | tf_op jit(solution)/shard_map/pick/pallas_call | solution.py:56
  1.9 8.7 %collective-permute-start = (bf16[4352,128]{1,0:T(8,128)(2,1)S(1)}, bf16[4352,128]{1,0:T(8,128)(2,1)S(1)}, u32[]{:S(2)}, u32[]{:S(2)}) collective-permute-start(bf16[4352,128]{1,0:T(8,128)(2,1)S(1)} %pick.1), channel_id=1, source_target_pairs={{0,8},{8,0},{1,9},{9,1},{2,10},{10,2},{3,11},{11,3},{4,12},{12,4},... | collective-permute-start | bytes 3342344 | tf_op jit(solution)/shard_map/ppermute | solution.py:178
  10.7 0.0 copy-done.1
  10.7 1.3 %constant_dynamic-slice_fusion.own_ref = bf16[4096,128]{1,0:T(8,128)(2,1)S(1)} fusion(bf16[8192,128]{1,0:T(8,128)(2,1)} %weight_ref.1, s32[]{:T(128)S(6)} %select_n.20), kind=kLoop, calls=%fused_computation.1 | loop fusion | bytes 2097156 | tf_op jit(solution)/shard_map/dynamic_slice | solution.py:177
  12.0 1.0 %collective-permute-done.swapped_ref = bf16[4352,128]{1,0:T(8,128)(2,1)S(1)} collective-permute-done((bf16[4352,128]{1,0:T(8,128)(2,1)S(1)}, bf16[4352,128]{1,0:T(8,128)(2,1)S(1)}, u32[]{:S(2)}, u32[]{:S(2)}) %collective-permute-start) | collective-permute-done | bytes 1114144 | tf_op jit(solution)/shard_map/ppermute | solution.py:178
  13.0 0.0 copy-done
  13.0 1.0 %partial.1 = bf16[4096,256]{1,0:T(8,128)(2,1)S(1)} custom-call(bf16[4096,128]{1,0:T(8,128)(2,1)S(1)} %constant_dynamic-slice_fusion.own_ref, bf16[4352,128]{1,0:T(8,128)(2,1)S(1)} %collective-permute-done.swapped_ref, bf16[256,128]{1,0:T(8,128)(2,1)S(1)} %copy-done), custom_call_target="tpu_custom_call" | custom-call | tf_op jit(solution)/shard_map/partial/pallas_call | solution.py:88
  14.0 29.5 %all_to_all.20.codes_ref = bf16[4,1024,256]{2,1,0:T(8,128)(2,1)S(1)} all-to-all(bf16[4,1024,256]{2,1,0:T(8,128)(2,1)S(1)} %bitcast.5), channel_id=1, replica_groups={{0,128,256,384},{16,144,272,400},{32,160,288,416},{48,176,304,432},{64,..., dimensions={0} | all-to-all | bytes 4194304 | tf_op jit(solution)/shard_map/all_to_all | solution.py:195
  43.5 1.4 %sum.1 = bf16[1024,256]{1,0:T(8,128)(2,1)S(1)} custom-call(bf16[4,1024,256]{2,1,0:T(8,128)(2,1)S(1)} %all_to_all.20.codes_ref), custom_call_target="tpu_custom_call" | custom-call | tf_op jit(solution)/shard_map/sum/pallas_call | solution.py:88
  44.9 23.3 %all_to_all.21.codes_ref = bf16[8,128,256]{2,1,0:T(8,128)(2,1)S(1)} all-to-all(bf16[8,128,256]{2,1,0:T(8,128)(2,1)S(1)} %bitcast.6), channel_id=1, replica_groups={{0,16,32,48,64,80,96,112},{128,144,160,176,192,208,224,240},{256,272,28..., dimensions={0} | all-to-all | bytes 1048576 | tf_op jit(solution)/shard_map/all_to_all | solution.py:200
  68.2 0.4 stats.1
  68.6 11.5 %all_to_all.22.parts_ref = f32[16,8,128]{2,1,0:T(8,128)S(1)} all-to-all(f32[16,8,128]{2,1,0:T(8,128)S(1)} %stats.1), channel_id=1, replica_groups=mesh['fsdp_0'=8,'fsdp_1'=4,'fsdp_2'=2,'tensor_0'=2,'tensor_1'=4] {'fsdp_..., dimensions={0} | all-to-all | bytes 131072 | tf_op jit(solution)/shard_map/all_to_all | solution.py:209
  80.1 14.9 %all_to_all.23.parts_ref = f32[32,8,128]{2,1,0:T(8,128)S(1)} all-to-all(f32[32,8,128]{2,1,0:T(8,128)S(1)} %combine.1), channel_id=1, replica_groups=mesh['fsdp_0'=8,'fsdp_1'=4,'fsdp_2'=2,'tensor_0'=2,'tensor_1'=4] {'tenso..., dimensions={0} | all-to-all | bytes 262144 | tf_op jit(solution)/shard_map/all_to_all | solution.py:213
  95.0 0.6 finish.1
  (2 shorter events, 0.0 us)
Async XLA Ops:
  0.6 12.4 %copy-start = (bf16[256,128]{1,0:T(8,128)(2,1)S(1)}, bf16[256,128]{1,0:T(8,128)(2,1)}, u32[]{:S(2)}) copy-start(bf16[256,128]{1,0:T(8,128)(2,1)} %hidden_ref.3) | copy-start | bytes 196612
  0.6 10.1 %copy-start.1 = (s32[256]{0:T(256)S(1)}, s32[256]{0:T(256)}, u32[]{:S(2)}) copy-start(s32[256]{0:T(256)} %param.5) | copy-start | bytes 3076
  1.9 11.1 %collective-permute-start = (bf16[4352,128]{1,0:T(8,128)(2,1)S(1)}, bf16[4352,128]{1,0:T(8,128)(2,1)S(1)}, u32[]{:S(2)}, u32[]{:S(2)}) collective-permute-start(bf16[4352,128]{1,0:T(8,128)(2,1)S(1)} %pick.1), channel_id=1, source_target_pairs={{0,8},{8,0},{1,9},{9,1},{2,10},{10,2},{3,11},{11,3},{4,12},{12,4},... | collective-permute-start | bytes 3342344 | tf_op jit(solution)/shard_map/ppermute | solution.py:178

commit v7 on v6

--- a/solution.py
+++ b/solution.py
@@ -12,8 +12,8 @@
 FSDP = (Z, Y, CORE)
 TENSOR = (YL, X)
 ALL = FSDP + TENSOR
-FIRST = (CORE, Z)
-SECOND = (X, YL, Y)
+FIRST = (CORE, X, YL)
+SECOND = (Z, Y)
 LANES = 128
 
 

time: 96.5 us -> 96.3 us (level)
  no operation moved by 1% of the time
where the time goes in v7:
time: 96.3 us; the launch traced here: 96 us
  blocking collectives  79.5 us (83%)
  starting transfers between devices  8.75 us (9%)
  Pallas kernels  4.68 us (5%)
  local copies, waits for them, and re-layouts  1.31 us (1%)
  waiting for transfers between devices  1 us (1%)
    all_to_all x1, blocking collectives, per_device(): codes = lax.all_to_all(codes, ALL, 0, 0, axis_index_groups=one)  29.5 us
    all_to_all x1, blocking collectives, per_device(): codes = lax.all_to_all(codes, ALL, 0, 0, axis_index_groups=two)  23.3 us
    all_to_all x1, blocking collectives, per_device(): stats = lax.all_to_all(stats, SECOND, 0, 0)  15.1 us
    all_to_all x1, blocking collectives, per_device(): stats = lax.all_to_all(stats, FIRST, 0, 0)  11.6 us
    ppermute x1, starting transfers between devices, per_device(): swapped = lax.ppermute(pick(head_weight, hidden), CORE, [(0, 1), (1, 0)])  8.75 us
    pallas_call x5, Pallas kernels, local_call(): pl.pallas_call(kernel, in_specs=specs, out_shape=results, name=name, comp...  3.41 us
  transfers between devices with their start and end apart: 1, of which 1 were waited for; matrix products, arithmetic and copies ran while one was open for 1% of the time, Pallas kernels for 0%

profile of v7, /device:TPU:1, one launch (start us, length us, event | category | flops | bytes accessed | tf_op | source)
XLA Modules:
  0.0 96.0 jit_solution(5937227396763859779)
XLA Ops:
  0.6 0.0 copy-start
  0.6 0.0 copy-start.1
  0.6 1.3 %pick.1 = bf16[4352,128]{1,0:T(8,128)(2,1)S(1)} custom-call(bf16[8192,128]{1,0:T(8,128)(2,1)} %weight_ref.1, bf16[256,128]{1,0:T(8,128)(2,1)} %hidden_ref.3), custom_call_target="tpu_custom_call" | custom-call | tf_op jit(solution)/shard_map/pick/pallas_call | solution.py:56
  1.9 8.7 %collective-permute-start = (bf16[4352,128]{1,0:T(8,128)(2,1)S(1)}, bf16[4352,128]{1,0:T(8,128)(2,1)S(1)}, u32[]{:S(2)}, u32[]{:S(2)}) collective-permute-start(bf16[4352,128]{1,0:T(8,128)(2,1)S(1)} %pick.1), channel_id=1, source_target_pairs={{0,8},{8,0},{1,9},{9,1},{2,10},{10,2},{3,11},{11,3},{4,12},{12,4},... | collective-permute-start | bytes 3342344 | tf_op jit(solution)/shard_map/ppermute | solution.py:178
  10.7 0.0 copy-done.1
  10.7 1.3 %constant_dynamic-slice_fusion.own_ref = bf16[4096,128]{1,0:T(8,128)(2,1)S(1)} fusion(bf16[8192,128]{1,0:T(8,128)(2,1)} %weight_ref.1, s32[]{:T(128)S(6)} %select_n.20), kind=kLoop, calls=%fused_computation.1 | loop fusion | bytes 2097156 | tf_op jit(solution)/shard_map/dynamic_slice | solution.py:177
  12.0 1.0 %collective-permute-done.swapped_ref = bf16[4352,128]{1,0:T(8,128)(2,1)S(1)} collective-permute-done((bf16[4352,128]{1,0:T(8,128)(2,1)S(1)}, bf16[4352,128]{1,0:T(8,128)(2,1)S(1)}, u32[]{:S(2)}, u32[]{:S(2)}) %collective-permute-start) | collective-permute-done | bytes 1114144 | tf_op jit(solution)/shard_map/ppermute | solution.py:178
  13.0 0.0 copy-done
  13.0 1.0 %partial.1 = bf16[4096,256]{1,0:T(8,128)(2,1)S(1)} custom-call(bf16[4096,128]{1,0:T(8,128)(2,1)S(1)} %constant_dynamic-slice_fusion.own_ref, bf16[4352,128]{1,0:T(8,128)(2,1)S(1)} %collective-permute-done.swapped_ref, bf16[256,128]{1,0:T(8,128)(2,1)S(1)} %copy-done), custom_call_target="tpu_custom_call" | custom-call | tf_op jit(solution)/shard_map/partial/pallas_call | solution.py:88
  14.0 29.5 %all_to_all.20.codes_ref = bf16[4,1024,256]{2,1,0:T(8,128)(2,1)S(1)} all-to-all(bf16[4,1024,256]{2,1,0:T(8,128)(2,1)S(1)} %bitcast.5), channel_id=1, replica_groups={{0,128,256,384},{16,144,272,400},{32,160,288,416},{48,176,304,432},{64,..., dimensions={0} | all-to-all | bytes 4194304 | tf_op jit(solution)/shard_map/all_to_all | solution.py:195
  43.5 1.4 %sum.1 = bf16[1024,256]{1,0:T(8,128)(2,1)S(1)} custom-call(bf16[4,1024,256]{2,1,0:T(8,128)(2,1)S(1)} %all_to_all.20.codes_ref), custom_call_target="tpu_custom_call" | custom-call | tf_op jit(solution)/shard_map/sum/pallas_call | solution.py:88
  44.9 23.3 %all_to_all.21.codes_ref = bf16[8,128,256]{2,1,0:T(8,128)(2,1)S(1)} all-to-all(bf16[8,128,256]{2,1,0:T(8,128)(2,1)S(1)} %bitcast.6), channel_id=1, replica_groups={{0,16,32,48,64,80,96,112},{128,144,160,176,192,208,224,240},{256,272,28..., dimensions={0} | all-to-all | bytes 1048576 | tf_op jit(solution)/shard_map/all_to_all | solution.py:200
  68.2 0.4 stats.1
  68.6 11.6 %all_to_all.22.parts_ref = f32[16,8,128]{2,1,0:T(8,128)S(1)} all-to-all(f32[16,8,128]{2,1,0:T(8,128)S(1)} %stats.1), channel_id=1, replica_groups=mesh['fsdp_0'=8,'fsdp_1'=4,'fsdp_2'=2,'tensor_0'=2,'tensor_1'=4] {'fsdp_..., dimensions={0} | all-to-all | bytes 131072 | tf_op jit(solution)/shard_map/all_to_all | solution.py:209
  80.2 15.1 %all_to_all.23.parts_ref = f32[32,8,128]{2,1,0:T(8,128)S(1)} all-to-all(f32[32,8,128]{2,1,0:T(8,128)S(1)} %combine.1), channel_id=1, replica_groups=mesh['fsdp_0'=8,'fsdp_1'=4,'fsdp_2'=2,'tensor_0'=2,'tensor_1'=4] {'fsdp_..., dimensions={0} | all-to-all | bytes 262144 | tf_op jit(solution)/shard_map/all_to_all | solution.py:213
  95.3 0.6 finish.1
  (2 shorter events, 0.0 us)
Async XLA Ops:
  0.6 12.4 %copy-start = (bf16[256,128]{1,0:T(8,128)(2,1)S(1)}, bf16[256,128]{1,0:T(8,128)(2,1)}, u32[]{:S(2)}) copy-start(bf16[256,128]{1,0:T(8,128)(2,1)} %hidden_ref.3) | copy-start | bytes 196612
  0.6 10.1 %copy-start.1 = (s32[256]{0:T(256)S(1)}, s32[256]{0:T(256)}, u32[]{:S(2)}) copy-start(s32[256]{0:T(256)} %param.5) | copy-start | bytes 3076
  1.9 11.1 %collective-permute-start = (bf16[4352,128]{1,0:T(8,128)(2,1)S(1)}, bf16[4352,128]{1,0:T(8,128)(2,1)S(1)}, u32[]{:S(2)}, u32[]{:S(2)}) collective-permute-start(bf16[4352,128]{1,0:T(8,128)(2,1)S(1)} %pick.1), channel_id=1, source_target_pairs={{0,8},{8,0},{1,9},{9,1},{2,10},{10,2},{3,11},{11,3},{4,12},{12,4},... | collective-permute-start | bytes 3342344 | tf_op jit(solution)/shard_map/ppermute | solution.py:178
